TPU v7x, 32 devices: a whole 2x2x4 slice. The times are simulated.
32 devices in a mesh: lat: 4 (over z), lon: 8 (over y, x, core).
Axes of the slice: x: 2, y: 2, z: 4, core: 2. Of those that a mesh axis runs over, the one named last changes fastest.
Arguments:
- fields: bfloat16 [3, 512, 32, 384], P(None, ('lat', 'lon')), may hold values from -6 to 6
- weights: bfloat16 [3, 1024, 8, 32, 128], P(None, ('lat', 'lon')), may hold values from -0.5 to 0.5
- pair_slots: int32 [3, 1024, 8], P(None, ('lat', 'lon')), may hold values from 0 to 15
- pair_counts: int32 [3, 1024], P(None, ('lat', 'lon')), may hold values from 1 to 8
- requests: int32 [3, 32, 16], replicated, may hold values from 0 to 511, as said below
- eofs: bfloat16 [200, 131072], P(None, ('lat', 'lon')), may hold values from -0.015625 to 0.015625
Outputs:
- pcs: float32 [200, 1152], P(None, ('lat', 'lon'))
Inputs may be any that keep to these rules, and one draw needn't show every extreme that they name: requests[g, d] lists 16 distinct source tiles for grid g and device d (d = lat index * lon devices + lon index); source tile j lies on device j // 16; all of them lie on devices with d's lat index whose lon index is d's own or one of its two cyclic neighbours, at most 8 on any one device, and exactly 8 on some device for every g and d. `pair_slots`: only entries with p < pair_counts[g, t] are used.
All inputs are finite; a program needn't handle non-finite values.
Results may differ from a plain program's by a relative error of at most 0.0029.
Values may be sent and summed in bfloat16 or wider, within the bound.
No kernel may reach another device: no remote copies, remote signals or barrier semaphores. Data moves between devices by JAX's collectives and lax.ppermute only.
A program may use at most 128 MiB of HBM per device.

v0:
```python
import functools

import jax
import jax.numpy as jnp
from jax import lax
from jax.experimental import pallas as pl
from jax.experimental.pallas import tpu as pltpu
from jax.sharding import PartitionSpec as P


MONTHS = 24
CORES = 2
MIB = 2**20

SMEM = pl.BlockSpec(memory_space=pltpu.SMEM)
VMEM = pl.BlockSpec(memory_space=pltpu.VMEM)
HBM = pl.BlockSpec(memory_space=pl.ANY)


def grant(size):
    return pltpu.CompilerParams(vmem_limit_bytes=size * MIB)


def stay(array):
    return pltpu.with_memory_space_constraint(array, pltpu.HBM)


def place():
    lat, lon, lon_count = lax.axis_index("lat"), lax.axis_index("lon"), lax.axis_size("lon")
    core = lax.rem(lon, CORES)
    pair = lon + 1 - 2 * core
    cross = lax.rem(lon + 2 * core - 1 + lon_count, lon_count)
    return lat, lon, pair, cross, lat * lon_count, lon_count


def list_tiles(requests, order, g, reader, owner, src_tiles):
    rank = jnp.int32(0)
    for r in range(requests.shape[1]):
        local = requests[g, r, reader] - owner * src_tiles
        hit = jnp.logical_and(local >= 0, local < src_tiles)
        order[rank] = jnp.where(hit, local, 0)
        rank += hit.astype(jnp.int32)
    return [jnp.where(j < rank, order[j], 0) for j in range(order.shape[0] - 1)]


def pick_kernel(requests_ref, fields_ref, out_ref, requests, fields, sems, *orders):
    _, lon, _, cross, base, _ = place()
    grids, src_tiles = fields.shape[:2]
    listing = pltpu.make_async_copy(requests_ref, requests, sems.at[grids])
    listing.start()
    loads = [pltpu.make_async_copy(fields_ref.at[g], fields.at[g], sems.at[g]) for g in range(grids)]
    for load in loads:
        load.start()
    listing.wait()
    listed = [
        list_tiles(requests, orders[g], g, base + cross, base + lon, src_tiles) for g in range(grids)
    ]
    for g in range(grids):
        loads[g].wait()
        for j, tile in enumerate(listed[g]):
            out_ref[g, j] = fields[g, tile]


def pick(requests, fields):
    grids, _, cells, columns = fields.shape
    cap = requests.shape[1] // 2
    return pl.pallas_call(
        pick_kernel,
        out_shape=jax.ShapeDtypeStruct((grids, cap, cells, columns), fields.dtype),
        in_specs=[HBM, HBM],
        out_specs=VMEM,
        scratch_shapes=[
            pltpu.SMEM(requests.shape, jnp.int32),
            pltpu.VMEM(fields.shape, fields.dtype),
            pltpu.SemaphoreType.DMA((grids + 1,)),
        ]
        + [pltpu.SMEM((cap + 1,), jnp.int32)] * grids,
        compiler_params=grant(6),
        name="pick",
    )(requests, fields)


def fold_kernel(src_tiles, requests, slots_ref, counts_ref, w_ref, e_ref, a_ref, where, *totals):
    step = pl.program_id(0)
    grids, tiles, depth, cells_x = w_ref.shape
    slots = requests.shape[1]
    cap = slots // 2
    pairs = slots_ref.shape[1]
    cells = depth // pairs
    eofs = e_ref.shape[0]
    lanes = a_ref.shape[2] // 2
    _, lon, pair, _, base, _ = place()

    @pl.when(step == 0)
    def _():
        for total in totals:
            total[...] = jnp.zeros_like(total)
        for g in range(grids):
            ranks = [jnp.int32(0)] * 3
            for r in range(slots):
                owner = lax.div(requests[g, r, base + lon], src_tiles) - base
                hits = [(owner == k).astype(jnp.int32) for k in (lon, pair)]
                hits.append(1 - hits[0] - hits[1])
                where[g, r] = sum(h * (k * cap + n) for k, (h, n) in enumerate(zip(hits, ranks)))
                ranks = [n + h for n, h in zip(ranks, hits)]

    for t in range(tiles):
        tile = step * tiles + t
        basis = e_ref[:, t * cells_x : (t + 1) * cells_x]
        parts = [
            lax.dot_general(
                w_ref[g, t], basis, (((1,), (1,)), ((), ())), preferred_element_type=jnp.float32
            )
            for g in range(grids)
        ]
        for p in range(pairs):
            for g in range(grids):
                spot = where[g, slots_ref[g, p, tile]]
                spot = jnp.where(p < counts_ref[g, tile], spot, 3 * cap)
                rows = pl.ds(pl.multiple_of(spot * cells, cells), cells)
                totals[g][rows, :] += parts[g][p * cells : (p + 1) * cells]

    @pl.when(step == pl.num_programs(0) - 1)
    def _():
        for g in range(grids):
            total = totals[g][: 3 * cap * cells, :]
            high = total.astype(jnp.bfloat16)
            low = (total - high.astype(jnp.float32)).astype(jnp.bfloat16)
            a_ref[g, :, :eofs] = high
            a_ref[g, :, lanes : lanes + eofs] = low


def fold(requests, slots, counts, weights, eofs, src_tiles):
    grids, tile_total, pairs, cells, cells_x = weights.shape
    cap = requests.shape[1] // 2
    lanes = pl.cdiv(eofs.shape[0], 128) * 128
    tiles = 4
    weights = stay(weights.reshape(grids, tile_total, pairs * cells, cells_x))
    flops = 2 * grids * tile_total * pairs * cells * cells_x * eofs.shape[0]
    return pl.pallas_call(
        functools.partial(fold_kernel, src_tiles),
        out_shape=jax.ShapeDtypeStruct((grids, 3 * cap * cells, 2 * lanes), jnp.bfloat16),
        grid=(tile_total // tiles,),
        in_specs=[
            SMEM,
            SMEM,
            SMEM,
            pl.BlockSpec((grids, tiles, pairs * cells, cells_x), lambda i: (0, i, 0, 0)),
            pl.BlockSpec((eofs.shape[0], tiles * cells_x), lambda i: (0, i)),
        ],
        out_specs=pl.BlockSpec((grids, 3 * cap * cells, 2 * lanes), lambda i: (0, 0, 0)),
        scratch_shapes=[pltpu.SMEM((grids, 2 * cap), jnp.int32)]
        + [pltpu.VMEM(((3 * cap + 1) * cells, eofs.shape[0]), jnp.float32)] * grids,
        cost_estimate=pl.CostEstimate(
            flops=8 * flops, bytes_accessed=weights.size * 2, transcendentals=0
        ),
        compiler_params=grant(20),
        name="fold",
    )(requests, slots, counts, weights, eofs)


def times(source, folded):
    return lax.dot_general(
        source, folded, (((0,), (0,)), ((), ())), preferred_element_type=jnp.float32
    )


def near_kernel(requests, fields, others, a_ref, near_ref, order, chosen):
    _, lon, pair, _, base, _ = place()
    grids, src_tiles, cells, columns = fields.shape
    cap = order.shape[0] - 1
    eofs = near_ref.shape[1]
    lanes = a_ref.shape[2] // 2
    for g in range(grids):
        for k, (owner, source) in enumerate(((lon, fields), (pair, others))):
            listed = list_tiles(requests, order, g, base + lon, base + owner, src_tiles)
            for j in range(cap):
                row = (k * cap + j) * cells
                chosen[row : row + cells, :] = source[g, listed[j]]
        total = times(chosen[...], a_ref[g, : 2 * cap * cells, :])
        near_ref[g * columns : (g + 1) * columns, :] = (
            total[:, :eofs] + total[:, lanes : lanes + eofs]
        )


def near(requests, fields, others, folded, eofs):
    grids, _, cells, columns = fields.shape
    cap = requests.shape[1] // 2
    return pl.pallas_call(
        near_kernel,
        out_shape=jax.ShapeDtypeStruct((grids * columns, eofs), jnp.float32),
        in_specs=[SMEM, VMEM, VMEM, VMEM],
        out_specs=VMEM,
        scratch_shapes=[
            pltpu.SMEM((cap + 1,), jnp.int32),
            pltpu.VMEM((2 * cap * cells, columns), fields.dtype),
        ],
        cost_estimate=pl.CostEstimate(flops=10**9, bytes_accessed=10**6, transcendentals=0),
        compiler_params=grant(12),
        name="near",
    )(requests, fields, others, folded)


def far_kernel(lat_count, near_ref, tiles, a_ref, keep_ref, send_ref, whole, units):
    lat, lon, _, _, _, lon_count = place()
    grids, cap, cells, columns = tiles.shape
    eofs = near_ref.shape[1]
    lanes = a_ref.shape[2] // 2
    planes = lon_count // CORES
    rows = units.shape[1]
    for g in range(grids):
        part = slice(g * columns, (g + 1) * columns)
        total = times(tiles[g].reshape(cap * cells, columns), a_ref[g, 2 * cap * cells :, :])
        product = near_ref[part, :] + total[:, :eofs] + total[:, lanes : lanes + eofs]
        product = product.reshape(columns // MONTHS, MONTHS, eofs)
        product = product - jnp.mean(product, axis=1, keepdims=True)
        whole[part, :] = product.reshape(columns, eofs)
    for u in range(units.shape[0]):
        units[u] = whole[u * rows : (u + 1) * rows, :]
    plane, core = lax.div(lon, CORES), lax.rem(lon, CORES)
    for c, out in ((0, keep_ref), (1, send_ref)):
        for r in range(planes):
            for q in range(lat_count):
                target = jnp.bitwise_xor(lat, q) * lon_count
                target += jnp.bitwise_xor(plane, r) * CORES + jnp.bitwise_xor(core, c)
                out[r, q * rows : (q + 1) * rows, :] = units[target]


def far(near_part, tiles, folded):
    lat_count, lon_count = lax.axis_size("lat"), lax.axis_size("lon")
    total_columns, eofs = near_part.shape
    rows = total_columns // (lat_count * lon_count)
    block = jax.ShapeDtypeStruct((lon_count // CORES, lat_count * rows, eofs), jnp.float32)
    return pl.pallas_call(
        functools.partial(far_kernel, lat_count),
        out_shape=(block, block),
        in_specs=[VMEM, VMEM, VMEM],
        out_specs=(VMEM, VMEM),
        scratch_shapes=[
            pltpu.VMEM((total_columns, eofs), jnp.float32),
            pltpu.VMEM((lat_count * lon_count, rows, eofs), jnp.float32),
        ],
        compiler_params=grant(16),
        name="far",
    )(near_part, tiles, folded)


def shards(fields, weights, pair_slots, pair_counts, requests, eofs):
    lat_count, lon_count = lax.axis_size("lat"), lax.axis_size("lon")
    planes = lon_count // CORES
    requests = stay(requests.transpose(0, 2, 1))
    pair_slots = stay(pair_slots.transpose(0, 2, 1))
    pair_counts = stay(pair_counts)
    eofs = stay(eofs)
    on_chip = [(i, i ^ 1) for i in range(lon_count)]
    off_chip = [(i, (i + 2 * (i % CORES) - 1) % lon_count) for i in range(lon_count)]
    picked, later = lax.optimization_barrier((pick(requests, stay(fields)), fields))
    tiles = lax.ppermute(picked, "lon", off_chip)
    others = lax.ppermute(later, "lon", on_chip)
    folded = fold(requests, pair_slots, pair_counts, weights, eofs, fields.shape[1])
    near_part = near(requests, fields, others, folded, eofs.shape[0])
    keep, send = far(near_part, tiles, folded)
    pair_sum = keep + lax.ppermute(send, "lon", on_chip)
    plane_sum = pair_sum[0]
    for r in reversed(range(1, planes)):
        swap = [(i, i ^ (r * CORES)) for i in range(lon_count)]
        sent = lax.ppermute(pair_sum[r].astype(jnp.bfloat16), "lon", swap)
        plane_sum = plane_sum + sent.astype(jnp.float32)
    rows = plane_sum.shape[0] // lat_count
    total = plane_sum[:rows]
    for q in reversed(range(1, lat_count)):
        swap = [(i, i ^ q) for i in range(lat_count)]
        total = total + lax.ppermute(plane_sum[q * rows : (q + 1) * rows], "lat", swap)
    return total.T


def solution(mesh):
    return jax.shard_map(
        shards,
        mesh=mesh,
        in_specs=(
            P(None, ("lat", "lon"), None, None),
            P(None, ("lat", "lon"), None, None, None),
            P(None, ("lat", "lon"), None),
            P(None, ("lat", "lon")),
            P(),
            P(None, ("lat", "lon")),
        ),
        out_specs=P(None, ("lat", "lon")),
        check_vma=False,
    )
```

profile of v0, /device:TPU:0, one launch (start us, length us, event | category | flops | bytes accessed | tf_op | source)
XLA Modules:
  0.0 39.0 jit_solution(14754081172365571594)
XLA Ops:
  0.0 1.5 %pick.1 = bf16[3,8,32,384]{3,2,1,0:T(8,128)(2,1)S(1)} custom-call(s32[3,16,32]{2,1,0:T(8,128)} %bitcast.19, bf16[3,16,32,384]{3,2,1,0:T(8,128)(2,1)} %fields.1), custom_call_target="tpu_custom_call" | custom-call | tf_op jit(solution)/shard_map/pick/pallas_call | solution.py:67
  1.5 0.1 copy-done
  1.6 0.5 %collective-permute-start = (bf16[3,16,32,384]{3,2,1,0:T(8,128)(2,1)S(1)}, bf16[3,16,32,384]{3,2,1,0:T(8,128)(2,1)S(1)}, u32[]{:S(2)}, u32[]{:S(2)}) collective-permute-start(bf16[3,16,32,384]{3,2,1,0:T(8,128)(2,1)S(1)} %copy-done), channel_id=1, source_target_pairs={{0,1},{1,0},{2,3},{3,2},{4,5},{5,4},{6,7},{7,6},{8,9},{9,8},{10,11... | collective-permute-start | bytes 3538952 | tf_op jit(solution)/shard_map/ppermute | solution.py:259
  2.1 3.5 %collective-permute-start.1 = (bf16[3,8,32,384]{3,2,1,0:T(8,128)(2,1)S(1)}, bf16[3,8,32,384]{3,2,1,0:T(8,128)(2,1)S(1)}, u32[]{:S(2)}, u32[]{:S(2)}) collective-permute-start(bf16[3,8,32,384]{3,2,1,0:T(8,128)(2,1)S(1)} %pick.1), channel_id=1, source_target_pairs={{0,7},{1,2},{2,1},{3,4},{4,3},{5,6},{6,5},{7,0},{8,15},{9,10},{10,... | collective-permute-start | bytes 1769480 | tf_op jit(solution)/shard_map/ppermute | solution.py:258
  5.7 9.5 %fold.1.a_ref = bf16[3,768,512]{2,1,0:T(8,128)(2,1)S(1)} custom-call(s32[3,16,32]{2,1,0:T(8,128)} %bitcast.20, s32[3,8,32]{2,1,0:T(8,128)} %bitcast.23, s32[3,32]{1,0:T(4,128)} %counts_ref.1, bf16[3,32,256,128]{3,2,1,0:T(8,128)(2,1)} %bitcast.22, bf16[200,4096]{1,0:T(8,128)(2,1)} %e_ref.1), custom_call_target="tpu_custom_call" | custom-call | flops 10066329600 | bytes 6291456 | tf_op jit(solution)/shard_map/fold/pallas_call | solution.py:140
  15.1 0.0 collective-permute-done.others
  15.2 2.2 %near.1.near_ref = f32[1152,200]{1,0:T(8,128)S(1)} custom-call(s32[3,16,32]{2,1,0:T(8,128)} %bitcast.21, bf16[3,16,32,384]{3,2,1,0:T(8,128)(2,1)S(1)} %copy-done, bf16[3,16,32,384]{3,2,1,0:T(8,128)(2,1)S(1)} %collective-permute-done.others, bf16[3,768,512]{2,1,0:T(8,128)(2,1)S(1)} %fold.1.a_ref), custom_call_target="tpu_custom_call" | custom-call | flops 1000000000 | bytes 1000000 | tf_op jit(solution)/shard_map/near/pallas_call | solution.py:189
  17.4 1.3 %collective-permute-done.1.tiles = bf16[3,8,32,384]{3,2,1,0:T(8,128)(2,1)S(1)} collective-permute-done((bf16[3,8,32,384]{3,2,1,0:T(8,128)(2,1)S(1)}, bf16[3,8,32,384]{3,2,1,0:T(8,128)(2,1)S(1)}, u32[]{:S(2)}, u32[]{:S(2)}) %collective-permute-start.1) | collective-permute-done | bytes 589856 | tf_op jit(solution)/shard_map/ppermute | solution.py:258
  18.7 0.8 %far.1 = (f32[4,144,200]{2,1,0:T(8,128)S(1)}, f32[4,144,200]{2,1,0:T(8,128)S(1)}) custom-call(f32[1152,200]{1,0:T(8,128)S(1)} %near.1.near_ref, bf16[3,8,32,384]{3,2,1,0:T(8,128)(2,1)S(1)} %collective-permute-done.1.tiles, bf16[3,768,512]{2,1,0:T(8,128)(2,1)S(1)} %fold.1.a_ref), custom_call_target="tpu_custom_call" | custom-call | tf_op jit(solution)/shard_map/far/pallas_call | solution.py:234
  19.5 0.1 collective-permute-start.2
  19.6 2.0 %collective-permute-done.2 = f32[4,144,200]{2,1,0:T(8,128)S(1)} collective-permute-done((f32[4,144,200]{2,1,0:T(8,128)S(1)}, f32[4,144,200]{2,1,0:T(8,128)S(1)}, u32[]{:S(2)}, u32[]{:S(2)}) %collective-permute-start.2) | collective-permute-done | bytes 460832 | tf_op jit(solution)/shard_map/ppermute | solution.py:263
  21.6 0.1 fusion.6
  21.7 1.9 %collective-permute-start.3 = (bf16[144,200]{1,0:T(8,128)(2,1)S(1)}, bf16[144,200]{1,0:T(8,128)(2,1)S(1)}, u32[]{:S(2)}, u32[]{:S(2)}) collective-permute-start(bf16[144,200]{1,0:T(8,128)(2,1)S(1)} %get-tuple-element.15), channel_id=1, source_target_pairs={{0,6},{1,7},{2,4},{3,5},{4,2},{5,3},{6,0},{7,1},{8,14},{9,15},{10,... | collective-permute-start | bytes 172808 | tf_op jit(solution)/shard_map/ppermute | solution.py:267
  23.6 1.1 %collective-permute-start.5 = (bf16[144,200]{1,0:T(8,128)(2,1)S(1)}, bf16[144,200]{1,0:T(8,128)(2,1)S(1)}, u32[]{:S(2)}, u32[]{:S(2)}) collective-permute-start(bf16[144,200]{1,0:T(8,128)(2,1)S(1)} %get-tuple-element.16), channel_id=1, source_target_pairs={{0,2},{1,3},{2,0},{3,1},{4,6},{5,7},{6,4},{7,5},{8,10},{9,11},{10,... | collective-permute-start | bytes 172808 | tf_op jit(solution)/shard_map/ppermute | solution.py:267
  24.7 0.5 %collective-permute-start.4 = (bf16[144,200]{1,0:T(8,128)(2,1)S(1)}, bf16[144,200]{1,0:T(8,128)(2,1)S(1)}, u32[]{:S(2)}, u32[]{:S(2)}) collective-permute-start(bf16[144,200]{1,0:T(8,128)(2,1)S(1)} %get-tuple-element.17), channel_id=1, source_target_pairs={{0,4},{1,5},{2,6},{3,7},{4,0},{5,1},{6,2},{7,3},{8,12},{9,13},{10,... | collective-permute-start | bytes 172808 | tf_op jit(solution)/shard_map/ppermute | solution.py:267
  25.2 1.8 %collective-permute-done.3 = bf16[144,200]{1,0:T(8,128)(2,1)S(1)} collective-permute-done((bf16[144,200]{1,0:T(8,128)(2,1)S(1)}, bf16[144,200]{1,0:T(8,128)(2,1)S(1)}, u32[]{:S(2)}, u32[]{:S(2)}) %collective-permute-start.3) | collective-permute-done | bytes 57632 | tf_op jit(solution)/shard_map/ppermute | solution.py:267
  27.0 1.6 %collective-permute-done.5 = bf16[144,200]{1,0:T(8,128)(2,1)S(1)} collective-permute-done((bf16[144,200]{1,0:T(8,128)(2,1)S(1)}, bf16[144,200]{1,0:T(8,128)(2,1)S(1)}, u32[]{:S(2)}, u32[]{:S(2)}) %collective-permute-start.5) | collective-permute-done | bytes 57632 | tf_op jit(solution)/shard_map/ppermute | solution.py:267
  28.6 0.4 %collective-permute-done.4 = bf16[144,200]{1,0:T(8,128)(2,1)S(1)} collective-permute-done((bf16[144,200]{1,0:T(8,128)(2,1)S(1)}, bf16[144,200]{1,0:T(8,128)(2,1)S(1)}, u32[]{:S(2)}, u32[]{:S(2)}) %collective-permute-start.4) | collective-permute-done | bytes 57632 | tf_op jit(solution)/shard_map/ppermute | solution.py:267
  29.2 4.3 %collective-permute-start.6 = (f32[36,200]{1,0:T(8,128)S(1)}, f32[36,200]{1,0:T(8,128)S(1)}, u32[]{:S(2)}, u32[]{:S(2)}) collective-permute-start(f32[36,200]{1,0:T(8,128)S(1)} %get-tuple-element.18), channel_id=1, source_target_pairs={{0,24},{8,16},{16,8},{24,0},{1,25},{9,17},{17,9},{25,1},{2,26},{10... | collective-permute-start | bytes 86408 | tf_op jit(solution)/shard_map/ppermute | solution.py:273
  33.5 0.6 %collective-permute-start.7 = (f32[36,200]{1,0:T(8,128)S(1)}, f32[36,200]{1,0:T(8,128)S(1)}, u32[]{:S(2)}, u32[]{:S(2)}) collective-permute-start(f32[36,200]{1,0:T(8,128)S(1)} %get-tuple-element.20), channel_id=1, source_target_pairs={{0,16},{8,24},{16,0},{24,8},{1,17},{9,25},{17,1},{25,9},{2,18},{10... | collective-permute-start | bytes 86408 | tf_op jit(solution)/shard_map/ppermute | solution.py:273
  34.1 1.4 %collective-permute-done.6 = f32[36,200]{1,0:T(8,128)S(1)} collective-permute-done((f32[36,200]{1,0:T(8,128)S(1)}, f32[36,200]{1,0:T(8,128)S(1)}, u32[]{:S(2)}, u32[]{:S(2)}) %collective-permute-start.6) | collective-permute-done | bytes 28832 | tf_op jit(solution)/shard_map/ppermute | solution.py:273
  35.5 2.0 %collective-permute-done.8 = f32[36,200]{1,0:T(8,128)S(1)} collective-permute-done((f32[36,200]{1,0:T(8,128)S(1)}, f32[36,200]{1,0:T(8,128)S(1)}, u32[]{:S(2)}, u32[]{:S(2)}) %collective-permute-start.8) | collective-permute-done | bytes 28832 | tf_op jit(solution)/shard_map/ppermute | solution.py:273
  37.5 0.9 %collective-permute-done.7 = f32[36,200]{1,0:T(8,128)S(1)} collective-permute-done((f32[36,200]{1,0:T(8,128)S(1)}, f32[36,200]{1,0:T(8,128)S(1)}, u32[]{:S(2)}, u32[]{:S(2)}) %collective-permute-start.7) | collective-permute-done | bytes 28832 | tf_op jit(solution)/shard_map/ppermute | solution.py:273
  38.4 0.6 %fusion.5 = f32[200,36]{0,1:T(8,128)} fusion(f32[36,200]{1,0:T(8,128)S(1)} %collective-permute-done.8, f32[36,200]{1,0:T(8,128)S(1)} %collective-permute-done.7, f32[36,200]{1,0:T(8,128)S(1)} %collective-permute-done.6, f32[144,200]{1,0:T(8,128)S(1)} %fusion.2), kind=kLoop, calls=%fused_computation.10 | loop fusion | flops 21600 | bytes 144000 | tf_op jit(solution)/shard_map/transpose | solution.py:274
  (5 shorter events, 0.1 us)
Async XLA Ops:
  0.0 1.6 %copy-start = (bf16[3,16,32,384]{3,2,1,0:T(8,128)(2,1)S(1)}, bf16[3,16,32,384]{3,2,1,0:T(8,128)(2,1)}, u32[]{:S(2)}) copy-start(bf16[3,16,32,384]{3,2,1,0:T(8,128)(2,1)} %fields.1) | copy-start | bytes 3538948
  1.6 13.5 %collective-permute-start = (bf16[3,16,32,384]{3,2,1,0:T(8,128)(2,1)S(1)}, bf16[3,16,32,384]{3,2,1,0:T(8,128)(2,1)S(1)}, u32[]{:S(2)}, u32[]{:S(2)}) collective-permute-start(bf16[3,16,32,384]{3,2,1,0:T(8,128)(2,1)S(1)} %copy-done), channel_id=1, source_target_pairs={{0,1},{1,0},{2,3},{3,2},{4,5},{5,4},{6,7},{7,6},{8,9},{9,8},{10,11... | collective-permute-start | bytes 3538952 | tf_op jit(solution)/shard_map/ppermute | solution.py:259
  2.1 16.6 %collective-permute-start.1 = (bf16[3,8,32,384]{3,2,1,0:T(8,128)(2,1)S(1)}, bf16[3,8,32,384]{3,2,1,0:T(8,128)(2,1)S(1)}, u32[]{:S(2)}, u32[]{:S(2)}) collective-permute-start(bf16[3,8,32,384]{3,2,1,0:T(8,128)(2,1)S(1)} %pick.1), channel_id=1, source_target_pairs={{0,7},{1,2},{2,1},{3,4},{4,3},{5,6},{6,5},{7,0},{8,15},{9,10},{10,... | collective-permute-start | bytes 1769480 | tf_op jit(solution)/shard_map/ppermute | solution.py:258
  19.5 2.1 %collective-permute-start.2 = (f32[4,144,200]{2,1,0:T(8,128)S(1)}, f32[4,144,200]{2,1,0:T(8,128)S(1)}, u32[]{:S(2)}, u32[]{:S(2)}) collective-permute-start(f32[4,144,200]{2,1,0:T(8,128)S(1)} %get-tuple-element.12), channel_id=1, source_target_pairs={{0,1},{1,0},{2,3},{3,2},{4,5},{5,4},{6,7},{7,6},{8,9},{9,8},{10,11... | collective-permute-start | bytes 1382408 | tf_op jit(solution)/shard_map/ppermute | solution.py:263
  21.7 5.3 %collective-permute-start.3 = (bf16[144,200]{1,0:T(8,128)(2,1)S(1)}, bf16[144,200]{1,0:T(8,128)(2,1)S(1)}, u32[]{:S(2)}, u32[]{:S(2)}) collective-permute-start(bf16[144,200]{1,0:T(8,128)(2,1)S(1)} %get-tuple-element.15), channel_id=1, source_target_pairs={{0,6},{1,7},{2,4},{3,5},{4,2},{5,3},{6,0},{7,1},{8,14},{9,15},{10,... | collective-permute-start | bytes 172808 | tf_op jit(solution)/shard_map/ppermute | solution.py:267
  23.6 5.0 %collective-permute-start.5 = (bf16[144,200]{1,0:T(8,128)(2,1)S(1)}, bf16[144,200]{1,0:T(8,128)(2,1)S(1)}, u32[]{:S(2)}, u32[]{:S(2)}) collective-permute-start(bf16[144,200]{1,0:T(8,128)(2,1)S(1)} %get-tuple-element.16), channel_id=1, source_target_pairs={{0,2},{1,3},{2,0},{3,1},{4,6},{5,7},{6,4},{7,5},{8,10},{9,11},{10,... | collective-permute-start | bytes 172808 | tf_op jit(solution)/shard_map/ppermute | solution.py:267
  24.7 4.4 %collective-permute-start.4 = (bf16[144,200]{1,0:T(8,128)(2,1)S(1)}, bf16[144,200]{1,0:T(8,128)(2,1)S(1)}, u32[]{:S(2)}, u32[]{:S(2)}) collective-permute-start(bf16[144,200]{1,0:T(8,128)(2,1)S(1)} %get-tuple-element.17), channel_id=1, source_target_pairs={{0,4},{1,5},{2,6},{3,7},{4,0},{5,1},{6,2},{7,3},{8,12},{9,13},{10,... | collective-permute-start | bytes 172808 | tf_op jit(solution)/shard_map/ppermute | solution.py:267
  29.2 6.3 %collective-permute-start.6 = (f32[36,200]{1,0:T(8,128)S(1)}, f32[36,200]{1,0:T(8,128)S(1)}, u32[]{:S(2)}, u32[]{:S(2)}) collective-permute-start(f32[36,200]{1,0:T(8,128)S(1)} %get-tuple-element.18), channel_id=1, source_target_pairs={{0,24},{8,16},{16,8},{24,0},{1,25},{9,17},{17,9},{25,1},{2,26},{10... | collective-permute-start | bytes 86408 | tf_op jit(solution)/shard_map/ppermute | solution.py:273
  33.5 4.0 %collective-permute-start.8 = (f32[36,200]{1,0:T(8,128)S(1)}, f32[36,200]{1,0:T(8,128)S(1)}, u32[]{:S(2)}, u32[]{:S(2)}) collective-permute-start(f32[36,200]{1,0:T(8,128)S(1)} %get-tuple-element.19), channel_id=1, source_target_pairs={{0,8},{8,0},{16,24},{24,16},{1,9},{9,1},{17,25},{25,17},{2,10},{10... | collective-permute-start | bytes 86408 | tf_op jit(solution)/shard_map/ppermute | solution.py:273
  33.5 4.9 %collective-permute-start.7 = (f32[36,200]{1,0:T(8,128)S(1)}, f32[36,200]{1,0:T(8,128)S(1)}, u32[]{:S(2)}, u32[]{:S(2)}) collective-permute-start(f32[36,200]{1,0:T(8,128)S(1)} %get-tuple-element.20), channel_id=1, source_target_pairs={{0,16},{8,24},{16,0},{24,8},{1,17},{9,25},{17,1},{25,9},{2,18},{10... | collective-permute-start | bytes 86408 | tf_op jit(solution)/shard_map/ppermute | solution.py:273
where the time goes:
time: 39.4 us; the launch traced here: 39 us
  Pallas kernels  14 us (36%)
  starting transfers between devices  12.6 us (32%)
  waiting for transfers between devices  11.4 us (29%)
  other arithmetic  0.75 us (2%)
    pallas_call x1, Pallas kernels, fold(): pl.pallas_call(functools.partial(fold_kernel, src_tiles), out_shape=jax.S...  9.47 us
    ppermute x3, starting transfers between devices, shards(): lax.ppermute(plane_sum[q * rows:(q + 1) * rows], 'lat', swap)  4.94 us
    ppermute x3, waiting for transfers between devices, shards(): lax.ppermute(plane_sum[q * rows:(q + 1) * rows], 'lat', swap)  4.26 us
    ppermute x3, waiting for transfers between devices, shards(): sent = lax.ppermute(pair_sum[r].astype(jnp.bfloat16), 'lon', swap)  3.86 us
    ppermute x3, starting transfers between devices, shards(): sent = lax.ppermute(pair_sum[r].astype(jnp.bfloat16), 'lon', swap)  3.55 us
    ppermute x1, starting transfers between devices, shards(): tiles = lax.ppermute(picked, 'lon', off_chip)  3.54 us
    pallas_call x1, Pallas kernels, near(): pl.pallas_call(near_kernel, out_shape=jax.ShapeDtypeStruct((grids * colum...  2.24 us
    ppermute x1, waiting for transfers between devices, shards(): pair_sum = keep + lax.ppermute(send, 'lon', on_chip)  1.99 us
  transfers between devices with their start and end apart: 9, of which 8 were waited for; matrix products, arithmetic and copies ran while one was open for 0% of the time, Pallas kernels for 30%

commit v1 on v0

--- a/solution.py
+++ b/solution.py
@@ -43,7 +43,7 @@
     return [jnp.where(j < rank, order[j], 0) for j in range(order.shape[0] - 1)]
 
 
-def pick_kernel(requests_ref, fields_ref, out_ref, requests, fields, sems, *orders):
+def pick_kernel(requests_ref, fields_ref, sent_ref, kept_ref, requests, fields, sems, *orders):
     _, lon, _, cross, base, _ = place()
     grids, src_tiles = fields.shape[:2]
     listing = pltpu.make_async_copy(requests_ref, requests, sems.at[grids])
@@ -58,7 +58,10 @@
     for g in range(grids):
         loads[g].wait()
         for j, tile in enumerate(listed[g]):
-            out_ref[g, j] = fields[g, tile]
+            if g < grids - 1:
+                sent_ref[g, j] = fields[g, tile]
+            else:
+                kept_ref[j] = fields[g, tile]
 
 
 def pick(requests, fields):
@@ -66,9 +69,12 @@
     cap = requests.shape[1] // 2
     return pl.pallas_call(
         pick_kernel,
-        out_shape=jax.ShapeDtypeStruct((grids, cap, cells, columns), fields.dtype),
+        out_shape=(
+            jax.ShapeDtypeStruct((grids - 1, cap, cells, columns), fields.dtype),
+            jax.ShapeDtypeStruct((cap, cells, columns), fields.dtype),
+        ),
         in_specs=[HBM, HBM],
-        out_specs=VMEM,
+        out_specs=(VMEM, VMEM),
         scratch_shapes=[
             pltpu.SMEM(requests.shape, jnp.int32),
             pltpu.VMEM(fields.shape, fields.dtype),
@@ -80,7 +86,9 @@
     )(requests, fields)
 
 
-def fold_kernel(src_tiles, requests, slots_ref, counts_ref, w_ref, e_ref, a_ref, where, *totals):
+def fold_kernel(
+    src_tiles, requests, slots_ref, counts_ref, w_ref, e_ref, a_ref, sent_ref, where, *totals
+):
     step = pl.program_id(0)
     grids, tiles, depth, cells_x = w_ref.shape
     slots = requests.shape[1]
@@ -128,18 +136,23 @@
             low = (total - high.astype(jnp.float32)).astype(jnp.bfloat16)
             a_ref[g, :, :eofs] = high
             a_ref[g, :, lanes : lanes + eofs] = low
+            if g == grids - 1:
+                sent_ref[...] = high[2 * cap * cells :, :]
 
 
 def fold(requests, slots, counts, weights, eofs, src_tiles):
     grids, tile_total, pairs, cells, cells_x = weights.shape
     cap = requests.shape[1] // 2
     lanes = pl.cdiv(eofs.shape[0], 128) * 128
-    tiles = 4
+    tiles = tile_total // 2
     weights = stay(weights.reshape(grids, tile_total, pairs * cells, cells_x))
     flops = 2 * grids * tile_total * pairs * cells * cells_x * eofs.shape[0]
     return pl.pallas_call(
         functools.partial(fold_kernel, src_tiles),
-        out_shape=jax.ShapeDtypeStruct((grids, 3 * cap * cells, 2 * lanes), jnp.bfloat16),
+        out_shape=(
+            jax.ShapeDtypeStruct((grids, 3 * cap * cells, 2 * lanes), jnp.bfloat16),
+            jax.ShapeDtypeStruct((cap * cells, eofs.shape[0]), jnp.bfloat16),
+        ),
         grid=(tile_total // tiles,),
         in_specs=[
             SMEM,
@@ -148,7 +161,10 @@
             pl.BlockSpec((grids, tiles, pairs * cells, cells_x), lambda i: (0, i, 0, 0)),
             pl.BlockSpec((eofs.shape[0], tiles * cells_x), lambda i: (0, i)),
         ],
-        out_specs=pl.BlockSpec((grids, 3 * cap * cells, 2 * lanes), lambda i: (0, 0, 0)),
+        out_specs=(
+            pl.BlockSpec((grids, 3 * cap * cells, 2 * lanes), lambda i: (0, 0, 0)),
+            pl.BlockSpec((cap * cells, eofs.shape[0]), lambda i: (0, 0)),
+        ),
         scratch_shapes=[pltpu.SMEM((grids, 2 * cap), jnp.int32)]
         + [pltpu.VMEM(((3 * cap + 1) * cells, eofs.shape[0]), jnp.float32)] * grids,
         cost_estimate=pl.CostEstimate(
@@ -201,17 +217,21 @@
     )(requests, fields, others, folded)
 
 
-def far_kernel(lat_count, near_ref, tiles, a_ref, keep_ref, send_ref, whole, units):
+def far_kernel(lat_count, near_ref, tiles, kept, a_ref, others_ref, keep_ref, send_ref, whole, units):
     lat, lon, _, _, _, lon_count = place()
-    grids, cap, cells, columns = tiles.shape
+    grids, cap, cells, columns = tiles.shape[0] + 1, *tiles.shape[1:]
     eofs = near_ref.shape[1]
     lanes = a_ref.shape[2] // 2
     planes = lon_count // CORES
     rows = units.shape[1]
     for g in range(grids):
         part = slice(g * columns, (g + 1) * columns)
-        total = times(tiles[g].reshape(cap * cells, columns), a_ref[g, 2 * cap * cells :, :])
-        product = near_ref[part, :] + total[:, :eofs] + total[:, lanes : lanes + eofs]
+        if g < grids - 1:
+            total = times(tiles[g].reshape(cap * cells, columns), a_ref[g, 2 * cap * cells :, :])
+            total = total[:, :eofs] + total[:, lanes : lanes + eofs]
+        else:
+            total = times(kept[...].reshape(cap * cells, columns), others_ref[...])
+        product = near_ref[part, :] + total
         product = product.reshape(columns // MONTHS, MONTHS, eofs)
         product = product - jnp.mean(product, axis=1, keepdims=True)
         whole[part, :] = product.reshape(columns, eofs)
@@ -226,7 +246,7 @@
                 out[r, q * rows : (q + 1) * rows, :] = units[target]
 
 
-def far(near_part, tiles, folded):
+def far(near_part, tiles, kept, folded, others):
     lat_count, lon_count = lax.axis_size("lat"), lax.axis_size("lon")
     total_columns, eofs = near_part.shape
     rows = total_columns // (lat_count * lon_count)
@@ -234,7 +254,7 @@
     return pl.pallas_call(
         functools.partial(far_kernel, lat_count),
         out_shape=(block, block),
-        in_specs=[VMEM, VMEM, VMEM],
+        in_specs=[VMEM] * 5,
         out_specs=(VMEM, VMEM),
         scratch_shapes=[
             pltpu.VMEM((total_columns, eofs), jnp.float32),
@@ -242,7 +262,7 @@
         ],
         compiler_params=grant(16),
         name="far",
-    )(near_part, tiles, folded)
+    )(near_part, tiles, kept, folded, others)
 
 
 def shards(fields, weights, pair_slots, pair_counts, requests, eofs):
@@ -254,12 +274,13 @@
     eofs = stay(eofs)
     on_chip = [(i, i ^ 1) for i in range(lon_count)]
     off_chip = [(i, (i + 2 * (i % CORES) - 1) % lon_count) for i in range(lon_count)]
-    picked, later = lax.optimization_barrier((pick(requests, stay(fields)), fields))
+    (picked, kept), later = lax.optimization_barrier((pick(requests, stay(fields)), fields))
     tiles = lax.ppermute(picked, "lon", off_chip)
     others = lax.ppermute(later, "lon", on_chip)
-    folded = fold(requests, pair_slots, pair_counts, weights, eofs, fields.shape[1])
+    folded, spread = fold(requests, pair_slots, pair_counts, weights, eofs, fields.shape[1])
+    spread = lax.ppermute(spread, "lon", off_chip)
     near_part = near(requests, fields, others, folded, eofs.shape[0])
-    keep, send = far(near_part, tiles, folded)
+    keep, send = far(near_part, tiles, kept, folded, spread)
     pair_sum = keep + lax.ppermute(send, "lon", on_chip)
     plane_sum = pair_sum[0]
     for r in reversed(range(1, planes)):

time: 39.4 us -> 37.7 us (0.957)
  Pallas kernels: 14 us -> 11.2 us
  waiting for transfers between devices: 11.4 us -> 13.2 us
    ppermute x0 -> x1, waiting for transfers between devices: none -> 3.76 us  [shards(): spread = lax.ppermute(spread, 'lon', off_chip)]
    pallas_call x2, Pallas kernels: 11 us -> 8.21 us  [the longest x1 6.86 us: fold(): pl.pallas_call(functools.partial(fold_kernel, src_tiles), out_shape=(jax....]
    ppermute x1, waiting for transfers between devices: 1.32 us -> 0.01 us  [shards(): tiles = lax.ppermute(picked, 'lon', off_chip)]
    ppermute x3, waiting for transfers between devices: 3.86 us -> 3.3 us  [shards(): sent = lax.ppermute(pair_sum[r].astype(jnp.bfloat16), 'lon', swap)]
    ppermute x3, starting transfers between devices: 4.94 us -> 4.45 us  [shards(): lax.ppermute(plane_sum[q * rows:(q + 1) * rows], 'lat', swap)]
  transfers between devices with their start and end apart: 9 -> 10, of which waited for: 8 -> 7; matrix products, arithmetic and copies ran while one was open for 0% -> 0% of each run, Pallas kernels for 30% -> 24%
where the time goes in v1:
time: 37.7 us; the launch traced here: 37.5 us
  waiting for transfers between devices  13.2 us (35%)
  starting transfers between devices  12.3 us (33%)
  Pallas kernels  11.2 us (30%)
  other arithmetic  0.75 us (2%)
    pallas_call x1, Pallas kernels, fold(): pl.pallas_call(functools.partial(fold_kernel, src_tiles), out_shape=(jax....  6.86 us
    ppermute x3, starting transfers between devices, shards(): lax.ppermute(plane_sum[q * rows:(q + 1) * rows], 'lat', swap)  4.45 us
    ppermute x3, waiting for transfers between devices, shards(): lax.ppermute(plane_sum[q * rows:(q + 1) * rows], 'lat', swap)  4.16 us
    ppermute x1, waiting for transfers between devices, shards(): spread = lax.ppermute(spread, 'lon', off_chip)  3.76 us
    ppermute x3, starting transfers between devices, shards(): sent = lax.ppermute(pair_sum[r].astype(jnp.bfloat16), 'lon', swap)  3.55 us
    ppermute x1, starting transfers between devices, shards(): tiles = lax.ppermute(picked, 'lon', off_chip)  3.54 us
    ppermute x3, waiting for transfers between devices, shards(): sent = lax.ppermute(pair_sum[r].astype(jnp.bfloat16), 'lon', swap)  3.3 us
    pallas_call x1, Pallas kernels, near(): pl.pallas_call(near_kernel, out_shape=jax.ShapeDtypeStruct((grids * colum...  2.24 us
  transfers between devices with their start and end apart: 10, of which 7 were waited for; matrix products, arithmetic and copies ran while one was open for 0% of the time, Pallas kernels for 24%

profile of v1, /device:TPU:0, one launch (start us, length us, event | category | flops | bytes accessed | tf_op | source)
XLA Modules:
  0.0 37.5 jit_solution(2982263916236617103)
XLA Ops:
  0.0 1.4 %pick.1 = (bf16[2,8,32,384]{3,2,1,0:T(8,128)(2,1)S(1)}, bf16[8,32,384]{2,1,0:T(8,128)(2,1)S(1)}) custom-call(s32[3,16,32]{2,1,0:T(8,128)} %bitcast.19, bf16[3,16,32,384]{3,2,1,0:T(8,128)(2,1)} %fields.1), custom_call_target="tpu_custom_call" | custom-call | tf_op jit(solution)/shard_map/pick/pallas_call | solution.py:70
  1.4 0.6 %collective-permute-start = (bf16[3,16,32,384]{3,2,1,0:T(8,128)(2,1)}, bf16[3,16,32,384]{3,2,1,0:T(8,128)(2,1)S(1)}, u32[]{:S(2)}, u32[]{:S(2)}) collective-permute-start(bf16[3,16,32,384]{3,2,1,0:T(8,128)(2,1)} %fields.1), channel_id=1, source_target_pairs={{0,1},{1,0},{2,3},{3,2},{4,5},{5,4},{6,7},{7,6},{8,9},{9,8},{10,11... | collective-permute-start | bytes 3538952 | tf_op jit(solution)/shard_map/ppermute | solution.py:279
  1.9 3.5 %collective-permute-start.1 = (bf16[2,8,32,384]{3,2,1,0:T(8,128)(2,1)S(1)}, bf16[2,8,32,384]{3,2,1,0:T(8,128)(2,1)S(1)}, u32[]{:S(2)}, u32[]{:S(2)}) collective-permute-start(bf16[2,8,32,384]{3,2,1,0:T(8,128)(2,1)S(1)} %get-tuple-element.18), channel_id=1, source_target_pairs={{0,7},{1,2},{2,1},{3,4},{4,3},{5,6},{6,5},{7,0},{8,15},{9,10},{10,... | collective-permute-start | bytes 1179656 | tf_op jit(solution)/shard_map/ppermute | solution.py:278
  5.5 6.9 %fold.1 = (bf16[3,768,512]{2,1,0:T(8,128)(2,1)S(1)}, bf16[256,200]{1,0:T(8,128)(2,1)S(1)}) custom-call(s32[3,16,32]{2,1,0:T(8,128)} %bitcast.20, s32[3,8,32]{2,1,0:T(8,128)} %bitcast.23, s32[3,32]{1,0:T(4,128)} %counts_ref.1, bf16[3,32,256,128]{3,2,1,0:T(8,128)(2,1)} %bitcast.22, bf16[200,4096]{1,0:T(8,128)(2,1)} %e_ref.1), custom_call_target="tpu_custom_call" | custom-call | flops 10066329600 | bytes 6291456 | tf_op jit(solution)/shard_map/fold/pallas_call | solution.py:150
  12.3 0.1 collective-permute-start.2
  12.4 0.0 collective-permute-done.others
  12.4 2.2 %near.1.near_ref = f32[1152,200]{1,0:T(8,128)S(1)} custom-call(s32[3,16,32]{2,1,0:T(8,128)} %bitcast.21, bf16[3,16,32,384]{3,2,1,0:T(8,128)(2,1)S(1)} %copy-done, bf16[3,16,32,384]{3,2,1,0:T(8,128)(2,1)S(1)} %collective-permute-done.others, bf16[3,768,512]{2,1,0:T(8,128)(2,1)S(1)} %get-tuple-element.17.a_ref), custom_call_target="tpu_custom_call" | custom-call | flops 1000000000 | bytes 1000000 | tf_op jit(solution)/shard_map/near/pallas_call | solution.py:205
  14.7 3.8 %collective-permute-done.2.others_ref = bf16[256,200]{1,0:T(8,128)(2,1)S(1)} collective-permute-done((bf16[256,200]{1,0:T(8,128)(2,1)S(1)}, bf16[256,200]{1,0:T(8,128)(2,1)S(1)}, u32[]{:S(2)}, u32[]{:S(2)}) %collective-permute-start.2) | collective-permute-done | bytes 102432 | tf_op jit(solution)/shard_map/ppermute | solution.py:281
  18.4 0.0 collective-permute-done.1.tiles
  18.4 0.7 %far.1 = (f32[4,144,200]{2,1,0:T(8,128)S(1)}, f32[4,144,200]{2,1,0:T(8,128)S(1)}) custom-call(f32[1152,200]{1,0:T(8,128)S(1)} %near.1.near_ref, bf16[2,8,32,384]{3,2,1,0:T(8,128)(2,1)S(1)} %collective-permute-done.1.tiles, bf16[8,32,384]{2,1,0:T(8,128)(2,1)S(1)} %get-tuple-element.19.kept, bf16[3,768,512]{2,1,0:T(8,128)(2,1)S(1)} %get-tuple-element.17.a_ref, ...), custom_call_target="tpu_custom_call" | custom-call | tf_op jit(solution)/shard_map/far/pallas_call | solution.py:254
  19.2 0.1 collective-permute-start.3
  19.3 2.0 %collective-permute-done.3 = f32[4,144,200]{2,1,0:T(8,128)S(1)} collective-permute-done((f32[4,144,200]{2,1,0:T(8,128)S(1)}, f32[4,144,200]{2,1,0:T(8,128)S(1)}, u32[]{:S(2)}, u32[]{:S(2)}) %collective-permute-start.3) | collective-permute-done | bytes 460832 | tf_op jit(solution)/shard_map/ppermute | solution.py:284
  21.3 0.1 fusion.6
  21.4 0.7 %collective-permute-start.4 = (bf16[144,200]{1,0:T(8,128)(2,1)S(1)}, bf16[144,200]{1,0:T(8,128)(2,1)S(1)}, u32[]{:S(2)}, u32[]{:S(2)}) collective-permute-start(bf16[144,200]{1,0:T(8,128)(2,1)S(1)} %get-tuple-element.25), channel_id=1, source_target_pairs={{0,6},{1,7},{2,4},{3,5},{4,2},{5,3},{6,0},{7,1},{8,14},{9,15},{10,... | collective-permute-start | bytes 172808 | tf_op jit(solution)/shard_map/ppermute | solution.py:288
  22.1 1.3 %collective-permute-start.6 = (bf16[144,200]{1,0:T(8,128)(2,1)S(1)}, bf16[144,200]{1,0:T(8,128)(2,1)S(1)}, u32[]{:S(2)}, u32[]{:S(2)}) collective-permute-start(bf16[144,200]{1,0:T(8,128)(2,1)S(1)} %get-tuple-element.26), channel_id=1, source_target_pairs={{0,2},{1,3},{2,0},{3,1},{4,6},{5,7},{6,4},{7,5},{8,10},{9,11},{10,... | collective-permute-start | bytes 172808 | tf_op jit(solution)/shard_map/ppermute | solution.py:288
  23.4 1.5 %collective-permute-start.5 = (bf16[144,200]{1,0:T(8,128)(2,1)S(1)}, bf16[144,200]{1,0:T(8,128)(2,1)S(1)}, u32[]{:S(2)}, u32[]{:S(2)}) collective-permute-start(bf16[144,200]{1,0:T(8,128)(2,1)S(1)} %get-tuple-element.27), channel_id=1, source_target_pairs={{0,4},{1,5},{2,6},{3,7},{4,0},{5,1},{6,2},{7,3},{8,12},{9,13},{10,... | collective-permute-start | bytes 172808 | tf_op jit(solution)/shard_map/ppermute | solution.py:288
  24.9 2.5 %collective-permute-done.4 = bf16[144,200]{1,0:T(8,128)(2,1)S(1)} collective-permute-done((bf16[144,200]{1,0:T(8,128)(2,1)S(1)}, bf16[144,200]{1,0:T(8,128)(2,1)S(1)}, u32[]{:S(2)}, u32[]{:S(2)}) %collective-permute-start.4) | collective-permute-done | bytes 57632 | tf_op jit(solution)/shard_map/ppermute | solution.py:288
  27.4 0.8 %collective-permute-done.5 = bf16[144,200]{1,0:T(8,128)(2,1)S(1)} collective-permute-done((bf16[144,200]{1,0:T(8,128)(2,1)S(1)}, bf16[144,200]{1,0:T(8,128)(2,1)S(1)}, u32[]{:S(2)}, u32[]{:S(2)}) %collective-permute-start.5) | collective-permute-done | bytes 57632 | tf_op jit(solution)/shard_map/ppermute | solution.py:288
  28.3 3.7 %collective-permute-start.7 = (f32[36,200]{1,0:T(8,128)S(1)}, f32[36,200]{1,0:T(8,128)S(1)}, u32[]{:S(2)}, u32[]{:S(2)}) collective-permute-start(f32[36,200]{1,0:T(8,128)S(1)} %get-tuple-element.28), channel_id=1, source_target_pairs={{0,24},{8,16},{16,8},{24,0},{1,25},{9,17},{17,9},{25,1},{2,26},{10... | collective-permute-start | bytes 86408 | tf_op jit(solution)/shard_map/ppermute | solution.py:294
  32.0 0.7 %collective-permute-start.8 = (f32[36,200]{1,0:T(8,128)S(1)}, f32[36,200]{1,0:T(8,128)S(1)}, u32[]{:S(2)}, u32[]{:S(2)}) collective-permute-start(f32[36,200]{1,0:T(8,128)S(1)} %get-tuple-element.30), channel_id=1, source_target_pairs={{0,16},{8,24},{16,0},{24,8},{1,17},{9,25},{17,1},{25,9},{2,18},{10... | collective-permute-start | bytes 86408 | tf_op jit(solution)/shard_map/ppermute | solution.py:294
  32.7 1.5 %collective-permute-done.7 = f32[36,200]{1,0:T(8,128)S(1)} collective-permute-done((f32[36,200]{1,0:T(8,128)S(1)}, f32[36,200]{1,0:T(8,128)S(1)}, u32[]{:S(2)}, u32[]{:S(2)}) %collective-permute-start.7) | collective-permute-done | bytes 28832 | tf_op jit(solution)/shard_map/ppermute | solution.py:294
  34.2 1.8 %collective-permute-done.9 = f32[36,200]{1,0:T(8,128)S(1)} collective-permute-done((f32[36,200]{1,0:T(8,128)S(1)}, f32[36,200]{1,0:T(8,128)S(1)}, u32[]{:S(2)}, u32[]{:S(2)}) %collective-permute-start.9) | collective-permute-done | bytes 28832 | tf_op jit(solution)/shard_map/ppermute | solution.py:294
  36.0 0.9 %collective-permute-done.8 = f32[36,200]{1,0:T(8,128)S(1)} collective-permute-done((f32[36,200]{1,0:T(8,128)S(1)}, f32[36,200]{1,0:T(8,128)S(1)}, u32[]{:S(2)}, u32[]{:S(2)}) %collective-permute-start.8) | collective-permute-done | bytes 28832 | tf_op jit(solution)/shard_map/ppermute | solution.py:294
  36.9 0.6 %fusion.5 = f32[200,36]{0,1:T(8,128)} fusion(f32[36,200]{1,0:T(8,128)S(1)} %collective-permute-done.9, f32[36,200]{1,0:T(8,128)S(1)} %collective-permute-done.8, f32[36,200]{1,0:T(8,128)S(1)} %collective-permute-done.7, f32[144,200]{1,0:T(8,128)S(1)} %fusion.2), kind=kLoop, calls=%fused_computation.10 | loop fusion | flops 21600 | bytes 144000 | tf_op jit(solution)/shard_map/transpose | solution.py:295
  (7 shorter events, 0.1 us)
Async XLA Ops:
  1.4 11.1 %collective-permute-start = (bf16[3,16,32,384]{3,2,1,0:T(8,128)(2,1)}, bf16[3,16,32,384]{3,2,1,0:T(8,128)(2,1)S(1)}, u32[]{:S(2)}, u32[]{:S(2)}) collective-permute-start(bf16[3,16,32,384]{3,2,1,0:T(8,128)(2,1)} %fields.1), channel_id=1, source_target_pairs={{0,1},{1,0},{2,3},{3,2},{4,5},{5,4},{6,7},{7,6},{8,9},{9,8},{10,11... | collective-permute-start | bytes 3538952 | tf_op jit(solution)/shard_map/ppermute | solution.py:279
  1.9 16.5 %collective-permute-start.1 = (bf16[2,8,32,384]{3,2,1,0:T(8,128)(2,1)S(1)}, bf16[2,8,32,384]{3,2,1,0:T(8,128)(2,1)S(1)}, u32[]{:S(2)}, u32[]{:S(2)}) collective-permute-start(bf16[2,8,32,384]{3,2,1,0:T(8,128)(2,1)S(1)} %get-tuple-element.18), channel_id=1, source_target_pairs={{0,7},{1,2},{2,1},{3,4},{4,3},{5,6},{6,5},{7,0},{8,15},{9,10},{10,... | collective-permute-start | bytes 1179656 | tf_op jit(solution)/shard_map/ppermute | solution.py:278
  5.5 7.0 %copy-start = (bf16[3,16,32,384]{3,2,1,0:T(8,128)(2,1)S(1)}, bf16[3,16,32,384]{3,2,1,0:T(8,128)(2,1)}, u32[]{:S(2)}) copy-start(bf16[3,16,32,384]{3,2,1,0:T(8,128)(2,1)} %fields.1) | copy-start | bytes 3538948
  12.3 6.1 %collective-permute-start.2 = (bf16[256,200]{1,0:T(8,128)(2,1)S(1)}, bf16[256,200]{1,0:T(8,128)(2,1)S(1)}, u32[]{:S(2)}, u32[]{:S(2)}) collective-permute-start(bf16[256,200]{1,0:T(8,128)(2,1)S(1)} %get-tuple-element.20), channel_id=1, source_target_pairs={{0,7},{1,2},{2,1},{3,4},{4,3},{5,6},{6,5},{7,0},{8,15},{9,10},{10,... | collective-permute-start | bytes 307208 | tf_op jit(solution)/shard_map/ppermute | solution.py:281
  19.2 2.1 %collective-permute-start.3 = (f32[4,144,200]{2,1,0:T(8,128)S(1)}, f32[4,144,200]{2,1,0:T(8,128)S(1)}, u32[]{:S(2)}, u32[]{:S(2)}) collective-permute-start(f32[4,144,200]{2,1,0:T(8,128)S(1)} %get-tuple-element.22), channel_id=1, source_target_pairs={{0,1},{1,0},{2,3},{3,2},{4,5},{5,4},{6,7},{7,6},{8,9},{9,8},{10,11... | collective-permute-start | bytes 1382408 | tf_op jit(solution)/shard_map/ppermute | solution.py:284
  21.4 6.1 %collective-permute-start.4 = (bf16[144,200]{1,0:T(8,128)(2,1)S(1)}, bf16[144,200]{1,0:T(8,128)(2,1)S(1)}, u32[]{:S(2)}, u32[]{:S(2)}) collective-permute-start(bf16[144,200]{1,0:T(8,128)(2,1)S(1)} %get-tuple-element.25), channel_id=1, source_target_pairs={{0,6},{1,7},{2,4},{3,5},{4,2},{5,3},{6,0},{7,1},{8,14},{9,15},{10,... | collective-permute-start | bytes 172808 | tf_op jit(solution)/shard_map/ppermute | solution.py:288
  22.1 5.3 %collective-permute-start.6 = (bf16[144,200]{1,0:T(8,128)(2,1)S(1)}, bf16[144,200]{1,0:T(8,128)(2,1)S(1)}, u32[]{:S(2)}, u32[]{:S(2)}) collective-permute-start(bf16[144,200]{1,0:T(8,128)(2,1)S(1)} %get-tuple-element.26), channel_id=1, source_target_pairs={{0,2},{1,3},{2,0},{3,1},{4,6},{5,7},{6,4},{7,5},{8,10},{9,11},{10,... | collective-permute-start | bytes 172808 | tf_op jit(solution)/shard_map/ppermute | solution.py:288
  23.4 4.8 %collective-permute-start.5 = (bf16[144,200]{1,0:T(8,128)(2,1)S(1)}, bf16[144,200]{1,0:T(8,128)(2,1)S(1)}, u32[]{:S(2)}, u32[]{:S(2)}) collective-permute-start(bf16[144,200]{1,0:T(8,128)(2,1)S(1)} %get-tuple-element.27), channel_id=1, source_target_pairs={{0,4},{1,5},{2,6},{3,7},{4,0},{5,1},{6,2},{7,3},{8,12},{9,13},{10,... | collective-permute-start | bytes 172808 | tf_op jit(solution)/shard_map/ppermute | solution.py:288
  28.3 5.9 %collective-permute-start.7 = (f32[36,200]{1,0:T(8,128)S(1)}, f32[36,200]{1,0:T(8,128)S(1)}, u32[]{:S(2)}, u32[]{:S(2)}) collective-permute-start(f32[36,200]{1,0:T(8,128)S(1)} %get-tuple-element.28), channel_id=1, source_target_pairs={{0,24},{8,16},{16,8},{24,0},{1,25},{9,17},{17,9},{25,1},{2,26},{10... | collective-permute-start | bytes 86408 | tf_op jit(solution)/shard_map/ppermute | solution.py:294
  32.0 4.0 %collective-permute-start.9 = (f32[36,200]{1,0:T(8,128)S(1)}, f32[36,200]{1,0:T(8,128)S(1)}, u32[]{:S(2)}, u32[]{:S(2)}) collective-permute-start(f32[36,200]{1,0:T(8,128)S(1)} %get-tuple-element.29), channel_id=1, source_target_pairs={{0,8},{8,0},{16,24},{24,16},{1,9},{9,1},{17,25},{25,17},{2,10},{10... | collective-permute-start | bytes 86408 | tf_op jit(solution)/shard_map/ppermute | solution.py:294
  32.0 4.9 %collective-permute-start.8 = (f32[36,200]{1,0:T(8,128)S(1)}, f32[36,200]{1,0:T(8,128)S(1)}, u32[]{:S(2)}, u32[]{:S(2)}) collective-permute-start(f32[36,200]{1,0:T(8,128)S(1)} %get-tuple-element.30), channel_id=1, source_target_pairs={{0,16},{8,24},{16,0},{24,8},{1,17},{9,25},{17,1},{25,9},{2,18},{10... | collective-permute-start | bytes 86408 | tf_op jit(solution)/shard_map/ppermute | solution.py:294

commit v2 on v1

--- a/solution.py
+++ b/solution.py
@@ -43,10 +43,10 @@
     return [jnp.where(j < rank, order[j], 0) for j in range(order.shape[0] - 1)]
 
 
-def pick_kernel(requests_ref, fields_ref, sent_ref, kept_ref, requests, fields, sems, *orders):
+def pick_kernel(requests_ref, fields_ref, sent_ref, requests, fields, sems, *orders):
     _, lon, _, cross, base, _ = place()
     grids, src_tiles = fields.shape[:2]
-    listing = pltpu.make_async_copy(requests_ref, requests, sems.at[grids])
+    listing = pltpu.make_async_copy(requests_ref.at[:grids], requests, sems.at[grids])
     listing.start()
     loads = [pltpu.make_async_copy(fields_ref.at[g], fields.at[g], sems.at[g]) for g in range(grids)]
     for load in loads:
@@ -58,26 +58,21 @@
     for g in range(grids):
         loads[g].wait()
         for j, tile in enumerate(listed[g]):
-            if g < grids - 1:
-                sent_ref[g, j] = fields[g, tile]
-            else:
-                kept_ref[j] = fields[g, tile]
+            sent_ref[g, j] = fields[g, tile]
 
 
 def pick(requests, fields):
-    grids, _, cells, columns = fields.shape
+    grids, src_tiles, cells, columns = fields.shape
+    grids -= 1
     cap = requests.shape[1] // 2
     return pl.pallas_call(
         pick_kernel,
-        out_shape=(
-            jax.ShapeDtypeStruct((grids - 1, cap, cells, columns), fields.dtype),
-            jax.ShapeDtypeStruct((cap, cells, columns), fields.dtype),
-        ),
+        out_shape=jax.ShapeDtypeStruct((grids, cap, cells, columns), fields.dtype),
         in_specs=[HBM, HBM],
-        out_specs=(VMEM, VMEM),
+        out_specs=VMEM,
         scratch_shapes=[
-            pltpu.SMEM(requests.shape, jnp.int32),
-            pltpu.VMEM(fields.shape, fields.dtype),
+            pltpu.SMEM((grids, *requests.shape[1:]), jnp.int32),
+            pltpu.VMEM((grids, src_tiles, cells, columns), fields.dtype),
             pltpu.SemaphoreType.DMA((grids + 1,)),
         ]
         + [pltpu.SMEM((cap + 1,), jnp.int32)] * grids,
@@ -137,7 +132,9 @@
             a_ref[g, :, :eofs] = high
             a_ref[g, :, lanes : lanes + eofs] = low
             if g == grids - 1:
-                sent_ref[...] = high[2 * cap * cells :, :]
+                for j in range(cap):
+                    row = (2 * cap + j) * cells
+                    sent_ref[:, j * eofs : (j + 1) * eofs] = high[row : row + cells, :]
 
 
 def fold(requests, slots, counts, weights, eofs, src_tiles):
@@ -151,7 +148,7 @@
         functools.partial(fold_kernel, src_tiles),
         out_shape=(
             jax.ShapeDtypeStruct((grids, 3 * cap * cells, 2 * lanes), jnp.bfloat16),
-            jax.ShapeDtypeStruct((cap * cells, eofs.shape[0]), jnp.bfloat16),
+            jax.ShapeDtypeStruct((cells, cap * eofs.shape[0]), jnp.bfloat16),
         ),
         grid=(tile_total // tiles,),
         in_specs=[
@@ -163,7 +160,7 @@
         ],
         out_specs=(
             pl.BlockSpec((grids, 3 * cap * cells, 2 * lanes), lambda i: (0, 0, 0)),
-            pl.BlockSpec((cap * cells, eofs.shape[0]), lambda i: (0, 0)),
+            pl.BlockSpec((cells, cap * eofs.shape[0]), lambda i: (0, 0)),
         ),
         scratch_shapes=[pltpu.SMEM((grids, 2 * cap), jnp.int32)]
         + [pltpu.VMEM(((3 * cap + 1) * cells, eofs.shape[0]), jnp.float32)] * grids,
@@ -181,8 +178,8 @@
     )
 
 
-def near_kernel(requests, fields, others, a_ref, near_ref, order, chosen):
-    _, lon, pair, _, base, _ = place()
+def near_kernel(requests, fields, others, a_ref, near_ref, kept_ref, order, chosen):
+    _, lon, pair, cross, base, _ = place()
     grids, src_tiles, cells, columns = fields.shape
     cap = order.shape[0] - 1
     eofs = near_ref.shape[1]
@@ -197,6 +194,11 @@
         near_ref[g * columns : (g + 1) * columns, :] = (
             total[:, :eofs] + total[:, lanes : lanes + eofs]
         )
+    last = grids - 1
+    for j, tile in enumerate(
+        list_tiles(requests, order, last, base + cross, base + lon, src_tiles)
+    ):
+        kept_ref[j * cells : (j + 1) * cells, :] = fields[last, tile]
 
 
 def near(requests, fields, others, folded, eofs):
@@ -204,9 +206,12 @@
     cap = requests.shape[1] // 2
     return pl.pallas_call(
         near_kernel,
-        out_shape=jax.ShapeDtypeStruct((grids * columns, eofs), jnp.float32),
+        out_shape=(
+            jax.ShapeDtypeStruct((grids * columns, eofs), jnp.float32),
+            jax.ShapeDtypeStruct((cap * cells, columns), fields.dtype),
+        ),
         in_specs=[SMEM, VMEM, VMEM, VMEM],
-        out_specs=VMEM,
+        out_specs=(VMEM, VMEM),
         scratch_shapes=[
             pltpu.SMEM((cap + 1,), jnp.int32),
             pltpu.VMEM((2 * cap * cells, columns), fields.dtype),
@@ -217,7 +222,9 @@
     )(requests, fields, others, folded)
 
 
-def far_kernel(lat_count, near_ref, tiles, kept, a_ref, others_ref, keep_ref, send_ref, whole, units):
+def far_kernel(
+    lat_count, near_ref, tiles, kept, a_ref, others_ref, keep_ref, send_ref, rows_of, whole, units
+):
     lat, lon, _, _, _, lon_count = place()
     grids, cap, cells, columns = tiles.shape[0] + 1, *tiles.shape[1:]
     eofs = near_ref.shape[1]
@@ -230,7 +237,9 @@
             total = times(tiles[g].reshape(cap * cells, columns), a_ref[g, 2 * cap * cells :, :])
             total = total[:, :eofs] + total[:, lanes : lanes + eofs]
         else:
-            total = times(kept[...].reshape(cap * cells, columns), others_ref[...])
+            for j in range(cap):
+                rows_of[j * cells : (j + 1) * cells, :] = others_ref[:, j * eofs : (j + 1) * eofs]
+            total = times(kept[...], rows_of[...])
         product = near_ref[part, :] + total
         product = product.reshape(columns // MONTHS, MONTHS, eofs)
         product = product - jnp.mean(product, axis=1, keepdims=True)
@@ -257,6 +266,7 @@
         in_specs=[VMEM] * 5,
         out_specs=(VMEM, VMEM),
         scratch_shapes=[
+            pltpu.VMEM((kept.shape[0], eofs), others.dtype),
             pltpu.VMEM((total_columns, eofs), jnp.float32),
             pltpu.VMEM((lat_count * lon_count, rows, eofs), jnp.float32),
         ],
@@ -274,12 +284,12 @@
     eofs = stay(eofs)
     on_chip = [(i, i ^ 1) for i in range(lon_count)]
     off_chip = [(i, (i + 2 * (i % CORES) - 1) % lon_count) for i in range(lon_count)]
-    (picked, kept), later = lax.optimization_barrier((pick(requests, stay(fields)), fields))
+    picked, later = lax.optimization_barrier((pick(requests, stay(fields)), fields))
     tiles = lax.ppermute(picked, "lon", off_chip)
     others = lax.ppermute(later, "lon", on_chip)
     folded, spread = fold(requests, pair_slots, pair_counts, weights, eofs, fields.shape[1])
     spread = lax.ppermute(spread, "lon", off_chip)
-    near_part = near(requests, fields, others, folded, eofs.shape[0])
+    near_part, kept = near(requests, fields, others, folded, eofs.shape[0])
     keep, send = far(near_part, tiles, kept, folded, spread)
     pair_sum = keep + lax.ppermute(send, "lon", on_chip)
     plane_sum = pair_sum[0]

time: 37.7 us -> 37.2 us (0.987)
  waiting for transfers between devices: 13.2 us -> 12.6 us
    ppermute x1, waiting for transfers between devices: 3.76 us -> 3.14 us  [shards(): spread = lax.ppermute(spread, 'lon', off_chip)]
  transfers between devices with their start and end apart: 10 -> 10, of which waited for: 7 -> 7; matrix products, arithmetic and copies ran while one was open for 0% -> 0% of each run, Pallas kernels for 24% -> 25%
where the time goes in v2:
time: 37.2 us; the launch traced here: 37 us
  waiting for transfers between devices  12.6 us (34%)
  starting transfers between devices  12.3 us (33%)
  Pallas kernels  11.3 us (30%)
  other arithmetic  0.79 us (2%)
    pallas_call x1, Pallas kernels, fold(): pl.pallas_call(functools.partial(fold_kernel, src_tiles), out_shape=(jax....  7.04 us
    ppermute x3, starting transfers between devices, shards(): lax.ppermute(plane_sum[q * rows:(q + 1) * rows], 'lat', swap)  4.45 us
    ppermute x3, waiting for transfers between devices, shards(): lax.ppermute(plane_sum[q * rows:(q + 1) * rows], 'lat', swap)  4.13 us
    ppermute x3, starting transfers between devices, shards(): sent = lax.ppermute(pair_sum[r].astype(jnp.bfloat16), 'lon', swap)  3.55 us
    ppermute x1, starting transfers between devices, shards(): tiles = lax.ppermute(picked, 'lon', off_chip)  3.54 us
    ppermute x3, waiting for transfers between devices, shards(): sent = lax.ppermute(pair_sum[r].astype(jnp.bfloat16), 'lon', swap)  3.3 us
    ppermute x1, waiting for transfers between devices, shards(): spread = lax.ppermute(spread, 'lon', off_chip)  3.14 us
    pallas_call x1, Pallas kernels, near(): pl.pallas_call(near_kernel, out_shape=(jax.ShapeDtypeStruct((grids * colu...  2.34 us
  transfers between devices with their start and end apart: 10, of which 7 were waited for; matrix products, arithmetic and copies ran while one was open for 0% of the time, Pallas kernels for 25%

profile of v2, /device:TPU:0, one launch (start us, length us, event | category | flops | bytes accessed | tf_op | source)
XLA Modules:
  0.0 37.0 jit_solution(17649184697065374213)
XLA Ops:
  0.0 1.2 %pick.1 = bf16[2,8,32,384]{3,2,1,0:T(8,128)(2,1)S(1)} custom-call(s32[3,16,32]{2,1,0:T(8,128)} %bitcast.19, bf16[3,16,32,384]{3,2,1,0:T(8,128)(2,1)} %fields.1), custom_call_target="tpu_custom_call" | custom-call | tf_op jit(solution)/shard_map/pick/pallas_call | solution.py:68
  1.2 0.6 %collective-permute-start = (bf16[3,16,32,384]{3,2,1,0:T(8,128)(2,1)}, bf16[3,16,32,384]{3,2,1,0:T(8,128)(2,1)S(1)}, u32[]{:S(2)}, u32[]{:S(2)}) collective-permute-start(bf16[3,16,32,384]{3,2,1,0:T(8,128)(2,1)} %fields.1), channel_id=1, source_target_pairs={{0,1},{1,0},{2,3},{3,2},{4,5},{5,4},{6,7},{7,6},{8,9},{9,8},{10,11... | collective-permute-start | bytes 3538952 | tf_op jit(solution)/shard_map/ppermute | solution.py:289
  1.7 3.5 %collective-permute-start.1 = (bf16[2,8,32,384]{3,2,1,0:T(8,128)(2,1)S(1)}, bf16[2,8,32,384]{3,2,1,0:T(8,128)(2,1)S(1)}, u32[]{:S(2)}, u32[]{:S(2)}) collective-permute-start(bf16[2,8,32,384]{3,2,1,0:T(8,128)(2,1)S(1)} %pick.1), channel_id=1, source_target_pairs={{0,7},{1,2},{2,1},{3,4},{4,3},{5,6},{6,5},{7,0},{8,15},{9,10},{10,... | collective-permute-start | bytes 1179656 | tf_op jit(solution)/shard_map/ppermute | solution.py:288
  5.3 7.0 %fold.1 = (bf16[3,768,512]{2,1,0:T(8,128)(2,1)S(1)}, bf16[32,1600]{1,0:T(8,128)(2,1)S(1)}) custom-call(s32[3,16,32]{2,1,0:T(8,128)} %bitcast.20, s32[3,8,32]{2,1,0:T(8,128)} %bitcast.23, s32[3,32]{1,0:T(4,128)} %counts_ref.1, bf16[3,32,256,128]{3,2,1,0:T(8,128)(2,1)} %bitcast.22, bf16[200,4096]{1,0:T(8,128)(2,1)} %e_ref.1), custom_call_target="tpu_custom_call" | custom-call | flops 10066329600 | bytes 6291456 | tf_op jit(solution)/shard_map/fold/pallas_call | solution.py:147
  12.3 0.1 collective-permute-start.2
  12.4 2.3 %near.1 = (f32[1152,200]{1,0:T(8,128)S(1)}, bf16[256,384]{1,0:T(8,128)(2,1)S(1)}) custom-call(s32[3,16,32]{2,1,0:T(8,128)} %bitcast.21, bf16[3,16,32,384]{3,2,1,0:T(8,128)(2,1)S(1)} %copy-done, bf16[3,16,32,384]{3,2,1,0:T(8,128)(2,1)S(1)} %collective-permute-done.others, bf16[3,768,512]{2,1,0:T(8,128)(2,1)S(1)} %get-tuple-element.14.a_ref), custom_call_target="tpu_custom_call" | custom-call | flops 1000000000 | bytes 1000000 | tf_op jit(solution)/shard_map/near/pallas_call | solution.py:207
  14.8 3.1 %collective-permute-done.2.others_ref = bf16[32,1600]{1,0:T(8,128)(2,1)S(1)} collective-permute-done((bf16[32,1600]{1,0:T(8,128)(2,1)S(1)}, bf16[32,1600]{1,0:T(8,128)(2,1)S(1)}, u32[]{:S(2)}, u32[]{:S(2)}) %collective-permute-start.2) | collective-permute-done | bytes 102432 | tf_op jit(solution)/shard_map/ppermute | solution.py:291
  17.9 0.0 collective-permute-done.1.tiles
  17.9 0.7 %far.1 = (f32[4,144,200]{2,1,0:T(8,128)S(1)}, f32[4,144,200]{2,1,0:T(8,128)S(1)}) custom-call(f32[1152,200]{1,0:T(8,128)S(1)} %get-tuple-element.15.near_ref, bf16[2,8,32,384]{3,2,1,0:T(8,128)(2,1)S(1)} %collective-permute-done.1.tiles, bf16[256,384]{1,0:T(8,128)(2,1)S(1)} %get-tuple-element.17.kept, bf16[3,768,512]{2,1,0:T(8,128)(2,1)S(1)} %get-tuple-element.14.a_ref, ...), custom_call_target="tpu_custom_call" | custom-call | tf_op jit(solution)/shard_map/far/pallas_call | solution.py:263
  18.7 0.1 collective-permute-start.3
  18.7 2.0 %collective-permute-done.3 = f32[4,144,200]{2,1,0:T(8,128)S(1)} collective-permute-done((f32[4,144,200]{2,1,0:T(8,128)S(1)}, f32[4,144,200]{2,1,0:T(8,128)S(1)}, u32[]{:S(2)}, u32[]{:S(2)}) %collective-permute-start.3) | collective-permute-done | bytes 460832 | tf_op jit(solution)/shard_map/ppermute | solution.py:294
  20.7 0.1 fusion.6
  20.9 0.5 %collective-permute-start.4 = (bf16[144,200]{1,0:T(8,128)(2,1)S(1)}, bf16[144,200]{1,0:T(8,128)(2,1)S(1)}, u32[]{:S(2)}, u32[]{:S(2)}) collective-permute-start(bf16[144,200]{1,0:T(8,128)(2,1)S(1)} %get-tuple-element.23), channel_id=1, source_target_pairs={{0,6},{1,7},{2,4},{3,5},{4,2},{5,3},{6,0},{7,1},{8,14},{9,15},{10,... | collective-permute-start | bytes 172808 | tf_op jit(solution)/shard_map/ppermute | solution.py:298
  21.4 1.5 %collective-permute-start.6 = (bf16[144,200]{1,0:T(8,128)(2,1)S(1)}, bf16[144,200]{1,0:T(8,128)(2,1)S(1)}, u32[]{:S(2)}, u32[]{:S(2)}) collective-permute-start(bf16[144,200]{1,0:T(8,128)(2,1)S(1)} %get-tuple-element.24), channel_id=1, source_target_pairs={{0,2},{1,3},{2,0},{3,1},{4,6},{5,7},{6,4},{7,5},{8,10},{9,11},{10,... | collective-permute-start | bytes 172808 | tf_op jit(solution)/shard_map/ppermute | solution.py:298
  22.9 1.5 %collective-permute-start.5 = (bf16[144,200]{1,0:T(8,128)(2,1)S(1)}, bf16[144,200]{1,0:T(8,128)(2,1)S(1)}, u32[]{:S(2)}, u32[]{:S(2)}) collective-permute-start(bf16[144,200]{1,0:T(8,128)(2,1)S(1)} %get-tuple-element.25), channel_id=1, source_target_pairs={{0,4},{1,5},{2,6},{3,7},{4,0},{5,1},{6,2},{7,3},{8,12},{9,13},{10,... | collective-permute-start | bytes 172808 | tf_op jit(solution)/shard_map/ppermute | solution.py:298
  24.4 2.5 %collective-permute-done.4 = bf16[144,200]{1,0:T(8,128)(2,1)S(1)} collective-permute-done((bf16[144,200]{1,0:T(8,128)(2,1)S(1)}, bf16[144,200]{1,0:T(8,128)(2,1)S(1)}, u32[]{:S(2)}, u32[]{:S(2)}) %collective-permute-start.4) | collective-permute-done | bytes 57632 | tf_op jit(solution)/shard_map/ppermute | solution.py:298
  26.9 0.0 collective-permute-done.6
  26.9 0.8 %collective-permute-done.5 = bf16[144,200]{1,0:T(8,128)(2,1)S(1)} collective-permute-done((bf16[144,200]{1,0:T(8,128)(2,1)S(1)}, bf16[144,200]{1,0:T(8,128)(2,1)S(1)}, u32[]{:S(2)}, u32[]{:S(2)}) %collective-permute-start.5) | collective-permute-done | bytes 57632 | tf_op jit(solution)/shard_map/ppermute | solution.py:298
  27.8 3.7 %collective-permute-start.7 = (f32[36,200]{1,0:T(8,128)S(1)}, f32[36,200]{1,0:T(8,128)S(1)}, u32[]{:S(2)}, u32[]{:S(2)}) collective-permute-start(f32[36,200]{1,0:T(8,128)S(1)} %get-tuple-element.26), channel_id=1, source_target_pairs={{0,24},{8,16},{16,8},{24,0},{1,25},{9,17},{17,9},{25,1},{2,26},{10... | collective-permute-start | bytes 86408 | tf_op jit(solution)/shard_map/ppermute | solution.py:304
  31.5 0.8 %collective-permute-start.8 = (f32[36,200]{1,0:T(8,128)S(1)}, f32[36,200]{1,0:T(8,128)S(1)}, u32[]{:S(2)}, u32[]{:S(2)}) collective-permute-start(f32[36,200]{1,0:T(8,128)S(1)} %get-tuple-element.28), channel_id=1, source_target_pairs={{0,16},{8,24},{16,0},{24,8},{1,17},{9,25},{17,1},{25,9},{2,18},{10... | collective-permute-start | bytes 86408 | tf_op jit(solution)/shard_map/ppermute | solution.py:304
  32.2 1.4 %collective-permute-done.7 = f32[36,200]{1,0:T(8,128)S(1)} collective-permute-done((f32[36,200]{1,0:T(8,128)S(1)}, f32[36,200]{1,0:T(8,128)S(1)}, u32[]{:S(2)}, u32[]{:S(2)}) %collective-permute-start.7) | collective-permute-done | bytes 28832 | tf_op jit(solution)/shard_map/ppermute | solution.py:304
  33.7 1.8 %collective-permute-done.9 = f32[36,200]{1,0:T(8,128)S(1)} collective-permute-done((f32[36,200]{1,0:T(8,128)S(1)}, f32[36,200]{1,0:T(8,128)S(1)}, u32[]{:S(2)}, u32[]{:S(2)}) %collective-permute-start.9) | collective-permute-done | bytes 28832 | tf_op jit(solution)/shard_map/ppermute | solution.py:304
  35.5 0.9 %collective-permute-done.8 = f32[36,200]{1,0:T(8,128)S(1)} collective-permute-done((f32[36,200]{1,0:T(8,128)S(1)}, f32[36,200]{1,0:T(8,128)S(1)}, u32[]{:S(2)}, u32[]{:S(2)}) %collective-permute-start.8) | collective-permute-done | bytes 28832 | tf_op jit(solution)/shard_map/ppermute | solution.py:304
  36.4 0.6 %fusion.5 = f32[200,36]{0,1:T(8,128)} fusion(f32[36,200]{1,0:T(8,128)S(1)} %collective-permute-done.9, f32[36,200]{1,0:T(8,128)S(1)} %collective-permute-done.8, f32[36,200]{1,0:T(8,128)S(1)} %collective-permute-done.7, f32[144,200]{1,0:T(8,128)S(1)} %fusion.2), kind=kLoop, calls=%fused_computation.10 | loop fusion | flops 21600 | bytes 144000 | tf_op jit(solution)/shard_map/transpose | solution.py:305
  (7 shorter events, 0.1 us)
Async XLA Ops:
  1.2 11.3 %collective-permute-start = (bf16[3,16,32,384]{3,2,1,0:T(8,128)(2,1)}, bf16[3,16,32,384]{3,2,1,0:T(8,128)(2,1)S(1)}, u32[]{:S(2)}, u32[]{:S(2)}) collective-permute-start(bf16[3,16,32,384]{3,2,1,0:T(8,128)(2,1)} %fields.1), channel_id=1, source_target_pairs={{0,1},{1,0},{2,3},{3,2},{4,5},{5,4},{6,7},{7,6},{8,9},{9,8},{10,11... | collective-permute-start | bytes 3538952 | tf_op jit(solution)/shard_map/ppermute | solution.py:289
  1.7 16.2 %collective-permute-start.1 = (bf16[2,8,32,384]{3,2,1,0:T(8,128)(2,1)S(1)}, bf16[2,8,32,384]{3,2,1,0:T(8,128)(2,1)S(1)}, u32[]{:S(2)}, u32[]{:S(2)}) collective-permute-start(bf16[2,8,32,384]{3,2,1,0:T(8,128)(2,1)S(1)} %pick.1), channel_id=1, source_target_pairs={{0,7},{1,2},{2,1},{3,4},{4,3},{5,6},{6,5},{7,0},{8,15},{9,10},{10,... | collective-permute-start | bytes 1179656 | tf_op jit(solution)/shard_map/ppermute | solution.py:288
  5.3 7.2 %copy-start = (bf16[3,16,32,384]{3,2,1,0:T(8,128)(2,1)S(1)}, bf16[3,16,32,384]{3,2,1,0:T(8,128)(2,1)}, u32[]{:S(2)}) copy-start(bf16[3,16,32,384]{3,2,1,0:T(8,128)(2,1)} %fields.1) | copy-start | bytes 3538948
  12.3 5.6 %collective-permute-start.2 = (bf16[32,1600]{1,0:T(8,128)(2,1)S(1)}, bf16[32,1600]{1,0:T(8,128)(2,1)S(1)}, u32[]{:S(2)}, u32[]{:S(2)}) collective-permute-start(bf16[32,1600]{1,0:T(8,128)(2,1)S(1)} %get-tuple-element.18), channel_id=1, source_target_pairs={{0,7},{1,2},{2,1},{3,4},{4,3},{5,6},{6,5},{7,0},{8,15},{9,10},{10,... | collective-permute-start | bytes 307208 | tf_op jit(solution)/shard_map/ppermute | solution.py:291
  18.7 2.1 %collective-permute-start.3 = (f32[4,144,200]{2,1,0:T(8,128)S(1)}, f32[4,144,200]{2,1,0:T(8,128)S(1)}, u32[]{:S(2)}, u32[]{:S(2)}) collective-permute-start(f32[4,144,200]{2,1,0:T(8,128)S(1)} %get-tuple-element.20), channel_id=1, source_target_pairs={{0,1},{1,0},{2,3},{3,2},{4,5},{5,4},{6,7},{7,6},{8,9},{9,8},{10,11... | collective-permute-start | bytes 1382408 | tf_op jit(solution)/shard_map/ppermute | solution.py:294
  20.9 6.1 %collective-permute-start.4 = (bf16[144,200]{1,0:T(8,128)(2,1)S(1)}, bf16[144,200]{1,0:T(8,128)(2,1)S(1)}, u32[]{:S(2)}, u32[]{:S(2)}) collective-permute-start(bf16[144,200]{1,0:T(8,128)(2,1)S(1)} %get-tuple-element.23), channel_id=1, source_target_pairs={{0,6},{1,7},{2,4},{3,5},{4,2},{5,3},{6,0},{7,1},{8,14},{9,15},{10,... | collective-permute-start | bytes 172808 | tf_op jit(solution)/shard_map/ppermute | solution.py:298
  21.4 5.5 %collective-permute-start.6 = (bf16[144,200]{1,0:T(8,128)(2,1)S(1)}, bf16[144,200]{1,0:T(8,128)(2,1)S(1)}, u32[]{:S(2)}, u32[]{:S(2)}) collective-permute-start(bf16[144,200]{1,0:T(8,128)(2,1)S(1)} %get-tuple-element.24), channel_id=1, source_target_pairs={{0,2},{1,3},{2,0},{3,1},{4,6},{5,7},{6,4},{7,5},{8,10},{9,11},{10,... | collective-permute-start | bytes 172808 | tf_op jit(solution)/shard_map/ppermute | solution.py:298
  22.9 4.8 %collective-permute-start.5 = (bf16[144,200]{1,0:T(8,128)(2,1)S(1)}, bf16[144,200]{1,0:T(8,128)(2,1)S(1)}, u32[]{:S(2)}, u32[]{:S(2)}) collective-permute-start(bf16[144,200]{1,0:T(8,128)(2,1)S(1)} %get-tuple-element.25), channel_id=1, source_target_pairs={{0,4},{1,5},{2,6},{3,7},{4,0},{5,1},{6,2},{7,3},{8,12},{9,13},{10,... | collective-permute-start | bytes 172808 | tf_op jit(solution)/shard_map/ppermute | solution.py:298
  27.8 5.9 %collective-permute-start.7 = (f32[36,200]{1,0:T(8,128)S(1)}, f32[36,200]{1,0:T(8,128)S(1)}, u32[]{:S(2)}, u32[]{:S(2)}) collective-permute-start(f32[36,200]{1,0:T(8,128)S(1)} %get-tuple-element.26), channel_id=1, source_target_pairs={{0,24},{8,16},{16,8},{24,0},{1,25},{9,17},{17,9},{25,1},{2,26},{10... | collective-permute-start | bytes 86408 | tf_op jit(solution)/shard_map/ppermute | solution.py:304
  31.5 4.0 %collective-permute-start.9 = (f32[36,200]{1,0:T(8,128)S(1)}, f32[36,200]{1,0:T(8,128)S(1)}, u32[]{:S(2)}, u32[]{:S(2)}) collective-permute-start(f32[36,200]{1,0:T(8,128)S(1)} %get-tuple-element.27), channel_id=1, source_target_pairs={{0,8},{8,0},{16,24},{24,16},{1,9},{9,1},{17,25},{25,17},{2,10},{10... | collective-permute-start | bytes 86408 | tf_op jit(solution)/shard_map/ppermute | solution.py:304
  31.5 4.9 %collective-permute-start.8 = (f32[36,200]{1,0:T(8,128)S(1)}, f32[36,200]{1,0:T(8,128)S(1)}, u32[]{:S(2)}, u32[]{:S(2)}) collective-permute-start(f32[36,200]{1,0:T(8,128)S(1)} %get-tuple-element.28), channel_id=1, source_target_pairs={{0,16},{8,24},{16,0},{24,8},{1,17},{9,25},{17,1},{25,9},{2,18},{10... | collective-permute-start | bytes 86408 | tf_op jit(solution)/shard_map/ppermute | solution.py:304

commit v3 on v2

--- a/solution.py
+++ b/solution.py
@@ -82,8 +82,9 @@
 
 
 def fold_kernel(
-    src_tiles, requests, slots_ref, counts_ref, w_ref, e_ref, a_ref, sent_ref, where, *totals
+    src_tiles, first, sends, requests, slots_ref, counts_ref, w_ref, e_ref, a_ref, *rest
 ):
+    sent_ref, where, *totals = rest if sends else (None, *rest)
     step = pl.program_id(0)
     grids, tiles, depth, cells_x = w_ref.shape
     slots = requests.shape[1]
@@ -92,6 +93,7 @@
     cells = depth // pairs
     eofs = e_ref.shape[0]
     lanes = a_ref.shape[2] // 2
+    chains = len(totals) // grids
     _, lon, pair, _, base, _ = place()
 
     @pl.when(step == 0)
@@ -101,7 +103,7 @@
         for g in range(grids):
             ranks = [jnp.int32(0)] * 3
             for r in range(slots):
-                owner = lax.div(requests[g, r, base + lon], src_tiles) - base
+                owner = lax.div(requests[first + g, r, base + lon], src_tiles) - base
                 hits = [(owner == k).astype(jnp.int32) for k in (lon, pair)]
                 hits.append(1 - hits[0] - hits[1])
                 where[g, r] = sum(h * (k * cap + n) for k, (h, n) in enumerate(zip(hits, ranks)))
@@ -118,56 +120,58 @@
         ]
         for p in range(pairs):
             for g in range(grids):
-                spot = where[g, slots_ref[g, p, tile]]
-                spot = jnp.where(p < counts_ref[g, tile], spot, 3 * cap)
+                spot = where[g, slots_ref[first + g, p, tile]]
+                spot = jnp.where(p < counts_ref[first + g, tile], spot, 3 * cap)
                 rows = pl.ds(pl.multiple_of(spot * cells, cells), cells)
-                totals[g][rows, :] += parts[g][p * cells : (p + 1) * cells]
+                total = totals[g * chains + p % chains]
+                total[rows, :] += parts[g][p * cells : (p + 1) * cells]
 
     @pl.when(step == pl.num_programs(0) - 1)
     def _():
         for g in range(grids):
-            total = totals[g][: 3 * cap * cells, :]
+            own = totals[g * chains : (g + 1) * chains]
+            total = sum(part[: 3 * cap * cells, :] for part in own)
             high = total.astype(jnp.bfloat16)
             low = (total - high.astype(jnp.float32)).astype(jnp.bfloat16)
             a_ref[g, :, :eofs] = high
             a_ref[g, :, lanes : lanes + eofs] = low
-            if g == grids - 1:
+            if sends:
                 for j in range(cap):
                     row = (2 * cap + j) * cells
                     sent_ref[:, j * eofs : (j + 1) * eofs] = high[row : row + cells, :]
 
 
-def fold(requests, slots, counts, weights, eofs, src_tiles):
-    grids, tile_total, pairs, cells, cells_x = weights.shape
+def fold(requests, slots, counts, weights, eofs, src_tiles, first, grids, sends):
+    tile_total, depth, cells_x = weights.shape[1:]
     cap = requests.shape[1] // 2
+    cells = depth // slots.shape[1]
     lanes = pl.cdiv(eofs.shape[0], 128) * 128
     tiles = tile_total // 2
-    weights = stay(weights.reshape(grids, tile_total, pairs * cells, cells_x))
-    flops = 2 * grids * tile_total * pairs * cells * cells_x * eofs.shape[0]
+    chains = 2 if sends else 1
+    flops = 2 * grids * tile_total * depth * cells_x * eofs.shape[0]
+    shapes = [jax.ShapeDtypeStruct((grids, 3 * cap * cells, 2 * lanes), jnp.bfloat16)]
+    blocks = [pl.BlockSpec((grids, 3 * cap * cells, 2 * lanes), lambda i: (0, 0, 0))]
+    if sends:
+        shapes.append(jax.ShapeDtypeStruct((cells, cap * eofs.shape[0]), jnp.bfloat16))
+        blocks.append(pl.BlockSpec((cells, cap * eofs.shape[0]), lambda i: (0, 0)))
     return pl.pallas_call(
-        functools.partial(fold_kernel, src_tiles),
-        out_shape=(
-            jax.ShapeDtypeStruct((grids, 3 * cap * cells, 2 * lanes), jnp.bfloat16),
-            jax.ShapeDtypeStruct((cells, cap * eofs.shape[0]), jnp.bfloat16),
-        ),
+        functools.partial(fold_kernel, src_tiles, first, sends),
+        out_shape=shapes,
         grid=(tile_total // tiles,),
         in_specs=[
             SMEM,
             SMEM,
             SMEM,
-            pl.BlockSpec((grids, tiles, pairs * cells, cells_x), lambda i: (0, i, 0, 0)),
+            pl.BlockSpec((grids, tiles, depth, cells_x), lambda i: (first // grids, i, 0, 0)),
             pl.BlockSpec((eofs.shape[0], tiles * cells_x), lambda i: (0, i)),
         ],
-        out_specs=(
-            pl.BlockSpec((grids, 3 * cap * cells, 2 * lanes), lambda i: (0, 0, 0)),
-            pl.BlockSpec((cells, cap * eofs.shape[0]), lambda i: (0, 0)),
+        out_specs=blocks,
+        scratch_shapes=[pltpu.SMEM((grids, 2 * cap), jnp.int32)]
+        + [pltpu.VMEM(((3 * cap + 1) * cells, eofs.shape[0]), jnp.float32)] * (grids * chains),
+        cost_estimate=pl.CostEstimate(
+            flops=8 * flops, bytes_accessed=grids * tile_total * depth * cells_x * 2, transcendentals=0
         ),
-        scratch_shapes=[pltpu.SMEM((grids, 2 * cap), jnp.int32)]
-        + [pltpu.VMEM(((3 * cap + 1) * cells, eofs.shape[0]), jnp.float32)] * grids,
-        cost_estimate=pl.CostEstimate(
-            flops=8 * flops, bytes_accessed=weights.size * 2, transcendentals=0
-        ),
-        compiler_params=grant(20),
+        compiler_params=grant(24),
         name="fold",
     )(requests, slots, counts, weights, eofs)
 
@@ -178,7 +182,7 @@
     )
 
 
-def near_kernel(requests, fields, others, a_ref, near_ref, kept_ref, order, chosen):
+def near_kernel(requests, fields, others, a_ref, last_ref, near_ref, kept_ref, order, chosen):
     _, lon, pair, cross, base, _ = place()
     grids, src_tiles, cells, columns = fields.shape
     cap = order.shape[0] - 1
@@ -190,7 +194,8 @@
             for j in range(cap):
                 row = (k * cap + j) * cells
                 chosen[row : row + cells, :] = source[g, listed[j]]
-        total = times(chosen[...], a_ref[g, : 2 * cap * cells, :])
+        weights = a_ref.at[g] if g < grids - 1 else last_ref.at[0]
+        total = times(chosen[...], weights[: 2 * cap * cells, :])
         near_ref[g * columns : (g + 1) * columns, :] = (
             total[:, :eofs] + total[:, lanes : lanes + eofs]
         )
@@ -201,7 +206,7 @@
         kept_ref[j * cells : (j + 1) * cells, :] = fields[last, tile]
 
 
-def near(requests, fields, others, folded, eofs):
+def near(requests, fields, others, folded, last, eofs):
     grids, _, cells, columns = fields.shape
     cap = requests.shape[1] // 2
     return pl.pallas_call(
@@ -210,7 +215,7 @@
             jax.ShapeDtypeStruct((grids * columns, eofs), jnp.float32),
             jax.ShapeDtypeStruct((cap * cells, columns), fields.dtype),
         ),
-        in_specs=[SMEM, VMEM, VMEM, VMEM],
+        in_specs=[SMEM, VMEM, VMEM, VMEM, VMEM],
         out_specs=(VMEM, VMEM),
         scratch_shapes=[
             pltpu.SMEM((cap + 1,), jnp.int32),
@@ -219,7 +224,7 @@
         cost_estimate=pl.CostEstimate(flops=10**9, bytes_accessed=10**6, transcendentals=0),
         compiler_params=grant(12),
         name="near",
-    )(requests, fields, others, folded)
+    )(requests, fields, others, folded, last)
 
 
 def far_kernel(
@@ -287,9 +292,13 @@
     picked, later = lax.optimization_barrier((pick(requests, stay(fields)), fields))
     tiles = lax.ppermute(picked, "lon", off_chip)
     others = lax.ppermute(later, "lon", on_chip)
-    folded, spread = fold(requests, pair_slots, pair_counts, weights, eofs, fields.shape[1])
+    grids, tile_total, pairs, cells, cells_x = weights.shape
+    weights = stay(weights.reshape(grids, tile_total, pairs * cells, cells_x))
+    tables = (requests, pair_slots, pair_counts, weights, eofs, fields.shape[1])
+    last, spread = fold(*tables, grids - 1, 1, True)
     spread = lax.ppermute(spread, "lon", off_chip)
-    near_part, kept = near(requests, fields, others, folded, eofs.shape[0])
+    (folded,) = fold(*tables, 0, grids - 1, False)
+    near_part, kept = near(requests, fields, others, folded, last, eofs.shape[0])
     keep, send = far(near_part, tiles, kept, folded, spread)
     pair_sum = keep + lax.ppermute(send, "lon", on_chip)
     plane_sum = pair_sum[0]

time: 37.2 us -> 37.2 us (level)
  waiting for transfers between devices: 12.6 us -> 10.1 us
  Pallas kernels: 11.3 us -> 13.1 us
    ppermute x1, waiting for transfers between devices: 3.14 us -> 0.01 us  [shards(): spread = lax.ppermute(spread, 'lon', off_chip)]
    pallas_call x1 -> x2, Pallas kernels: 7.04 us -> 8.72 us  [fold(): pl.pallas_call(functools.partial(fold_kernel, src_tiles, first, sends), o...]
    ppermute x3, waiting for transfers between devices: 3.3 us -> 3.85 us  [shards(): sent = lax.ppermute(pair_sum[r].astype(jnp.bfloat16), 'lon', swap)]
    ppermute x3, starting transfers between devices: 4.45 us -> 4.87 us  [shards(): lax.ppermute(plane_sum[q * rows:(q + 1) * rows], 'lat', swap)]
  transfers between devices with their start and end apart: 10 -> 10, of which waited for: 7 -> 7; matrix products, arithmetic and copies ran while one was open for 0% -> 0% of each run, Pallas kernels for 25% -> 30%
where the time goes in v3:
time: 37.2 us; the launch traced here: 36.9 us
  Pallas kernels  13.1 us (35%)
  starting transfers between devices  12.6 us (34%)
  waiting for transfers between devices  10.1 us (27%)
  other arithmetic  0.79 us (2%)
    pallas_call x2, Pallas kernels, fold(): pl.pallas_call(functools.partial(fold_kernel, src_tiles, first, sends), o...  8.72 us
    ppermute x3, starting transfers between devices, shards(): lax.ppermute(plane_sum[q * rows:(q + 1) * rows], 'lat', swap)  4.87 us
    ppermute x3, waiting for transfers between devices, shards(): lax.ppermute(plane_sum[q * rows:(q + 1) * rows], 'lat', swap)  4.26 us
    ppermute x3, waiting for transfers between devices, shards(): sent = lax.ppermute(pair_sum[r].astype(jnp.bfloat16), 'lon', swap)  3.85 us
    ppermute x3, starting transfers between devices, shards(): sent = lax.ppermute(pair_sum[r].astype(jnp.bfloat16), 'lon', swap)  3.55 us
    ppermute x1, starting transfers between devices, shards(): tiles = lax.ppermute(picked, 'lon', off_chip)  3.54 us
    pallas_call x1, Pallas kernels, near(): pl.pallas_call(near_kernel, out_shape=(jax.ShapeDtypeStruct((grids * colu...  2.34 us
    ppermute x1, waiting for transfers between devices, shards(): pair_sum = keep + lax.ppermute(send, 'lon', on_chip)  1.99 us
  transfers between devices with their start and end apart: 10, of which 7 were waited for; matrix products, arithmetic and copies ran while one was open for 0% of the time, Pallas kernels for 30%

profile of v3, /device:TPU:0, one launch (start us, length us, event | category | flops | bytes accessed | tf_op | source)
XLA Modules:
  0.0 36.9 jit_solution(17656882678920921552)
XLA Ops:
  0.0 1.3 %pick.1 = bf16[2,8,32,384]{3,2,1,0:T(8,128)(2,1)S(1)} custom-call(s32[3,16,32]{2,1,0:T(8,128)} %bitcast.19, bf16[3,16,32,384]{3,2,1,0:T(8,128)(2,1)} %fields.1), custom_call_target="tpu_custom_call" | custom-call | tf_op jit(solution)/shard_map/pick/pallas_call | solution.py:68
  1.3 0.2 copy-done
  1.5 0.5 %collective-permute-start = (bf16[3,16,32,384]{3,2,1,0:T(8,128)(2,1)S(1)}, bf16[3,16,32,384]{3,2,1,0:T(8,128)(2,1)S(1)}, u32[]{:S(2)}, u32[]{:S(2)}) collective-permute-start(bf16[3,16,32,384]{3,2,1,0:T(8,128)(2,1)S(1)} %copy-done), channel_id=1, source_target_pairs={{0,1},{1,0},{2,3},{3,2},{4,5},{5,4},{6,7},{7,6},{8,9},{9,8},{10,11... | collective-permute-start | bytes 3538952 | tf_op jit(solution)/shard_map/ppermute | solution.py:294
  2.0 3.5 %collective-permute-start.1 = (bf16[2,8,32,384]{3,2,1,0:T(8,128)(2,1)S(1)}, bf16[2,8,32,384]{3,2,1,0:T(8,128)(2,1)S(1)}, u32[]{:S(2)}, u32[]{:S(2)}) collective-permute-start(bf16[2,8,32,384]{3,2,1,0:T(8,128)(2,1)S(1)} %pick.1), channel_id=1, source_target_pairs={{0,7},{1,2},{2,1},{3,4},{4,3},{5,6},{6,5},{7,0},{8,15},{9,10},{10,... | collective-permute-start | bytes 1179656 | tf_op jit(solution)/shard_map/ppermute | solution.py:293
  5.5 3.6 %fold.3 = (bf16[1,768,512]{2,1,0:T(8,128)(2,1)S(1)}, bf16[32,1600]{1,0:T(8,128)(2,1)S(1)}) custom-call(s32[3,16,32]{2,1,0:T(8,128)} %bitcast.20, s32[3,8,32]{2,1,0:T(8,128)} %bitcast.25, s32[3,32]{1,0:T(4,128)} %counts_ref.3, bf16[3,32,256,128]{3,2,1,0:T(8,128)(2,1)} %bitcast.23, bf16[200,4096]{1,0:T(8,128)(2,1)} %e_ref.3), custom_call_target="tpu_custom_call" | custom-call | flops 3355443200 | bytes 2097152 | tf_op jit(solution)/shard_map/fold/pallas_call | solution.py:157
  9.2 0.1 collective-permute-start.2
  9.3 5.1 %fold.2.a_ref = bf16[2,768,512]{2,1,0:T(8,128)(2,1)S(1)} custom-call(s32[3,16,32]{2,1,0:T(8,128)} %bitcast.21, s32[3,8,32]{2,1,0:T(8,128)} %bitcast.26, s32[3,32]{1,0:T(4,128)} %counts_ref.3, bf16[3,32,256,128]{3,2,1,0:T(8,128)(2,1)} %bitcast.24, bf16[200,4096]{1,0:T(8,128)(2,1)} %e_ref.3), custom_call_target="tpu_custom_call" | custom-call | flops 6710886400 | bytes 4194304 | tf_op jit(solution)/shard_map/fold/pallas_call | solution.py:157
  14.4 2.3 %near.1 = (f32[1152,200]{1,0:T(8,128)S(1)}, bf16[256,384]{1,0:T(8,128)(2,1)S(1)}) custom-call(s32[3,16,32]{2,1,0:T(8,128)} %bitcast.22, bf16[3,16,32,384]{3,2,1,0:T(8,128)(2,1)S(1)} %copy-done, bf16[3,16,32,384]{3,2,1,0:T(8,128)(2,1)S(1)} %collective-permute-done.others, bf16[2,768,512]{2,1,0:T(8,128)(2,1)S(1)} %fold.2.a_ref, ...), custom_call_target="tpu_custom_call" | custom-call | flops 1000000000 | bytes 1000000 | tf_op jit(solution)/shard_map/near/pallas_call | solution.py:212
  16.7 0.7 %far.1 = (f32[4,144,200]{2,1,0:T(8,128)S(1)}, f32[4,144,200]{2,1,0:T(8,128)S(1)}) custom-call(f32[1152,200]{1,0:T(8,128)S(1)} %get-tuple-element.15.near_ref, bf16[2,8,32,384]{3,2,1,0:T(8,128)(2,1)S(1)} %collective-permute-done.1.tiles, bf16[256,384]{1,0:T(8,128)(2,1)S(1)} %get-tuple-element.17.kept, bf16[2,768,512]{2,1,0:T(8,128)(2,1)S(1)} %fold.2.a_ref, ...), custom_call_target="tpu_custom_call" | custom-call | tf_op jit(solution)/shard_map/far/pallas_call | solution.py:268
  17.5 0.1 collective-permute-start.3
  17.6 2.0 %collective-permute-done.3 = f32[4,144,200]{2,1,0:T(8,128)S(1)} collective-permute-done((f32[4,144,200]{2,1,0:T(8,128)S(1)}, f32[4,144,200]{2,1,0:T(8,128)S(1)}, u32[]{:S(2)}, u32[]{:S(2)}) %collective-permute-start.3) | collective-permute-done | bytes 460832 | tf_op jit(solution)/shard_map/ppermute | solution.py:303
  19.6 0.1 fusion.6
  19.7 2.7 %collective-permute-start.4 = (bf16[144,200]{1,0:T(8,128)(2,1)S(1)}, bf16[144,200]{1,0:T(8,128)(2,1)S(1)}, u32[]{:S(2)}, u32[]{:S(2)}) collective-permute-start(bf16[144,200]{1,0:T(8,128)(2,1)S(1)} %get-tuple-element.23), channel_id=1, source_target_pairs={{0,6},{1,7},{2,4},{3,5},{4,2},{5,3},{6,0},{7,1},{8,14},{9,15},{10,... | collective-permute-start | bytes 172808 | tf_op jit(solution)/shard_map/ppermute | solution.py:307
  22.4 0.4 %collective-permute-start.6 = (bf16[144,200]{1,0:T(8,128)(2,1)S(1)}, bf16[144,200]{1,0:T(8,128)(2,1)S(1)}, u32[]{:S(2)}, u32[]{:S(2)}) collective-permute-start(bf16[144,200]{1,0:T(8,128)(2,1)S(1)} %get-tuple-element.24), channel_id=1, source_target_pairs={{0,2},{1,3},{2,0},{3,1},{4,6},{5,7},{6,4},{7,5},{8,10},{9,11},{10,... | collective-permute-start | bytes 172808 | tf_op jit(solution)/shard_map/ppermute | solution.py:307
  22.8 0.5 %collective-permute-start.5 = (bf16[144,200]{1,0:T(8,128)(2,1)S(1)}, bf16[144,200]{1,0:T(8,128)(2,1)S(1)}, u32[]{:S(2)}, u32[]{:S(2)}) collective-permute-start(bf16[144,200]{1,0:T(8,128)(2,1)S(1)} %get-tuple-element.25), channel_id=1, source_target_pairs={{0,4},{1,5},{2,6},{3,7},{4,0},{5,1},{6,2},{7,3},{8,12},{9,13},{10,... | collective-permute-start | bytes 172808 | tf_op jit(solution)/shard_map/ppermute | solution.py:307
  23.3 1.9 %collective-permute-done.4 = bf16[144,200]{1,0:T(8,128)(2,1)S(1)} collective-permute-done((bf16[144,200]{1,0:T(8,128)(2,1)S(1)}, bf16[144,200]{1,0:T(8,128)(2,1)S(1)}, u32[]{:S(2)}, u32[]{:S(2)}) %collective-permute-start.4) | collective-permute-done | bytes 57632 | tf_op jit(solution)/shard_map/ppermute | solution.py:307
  25.2 1.5 %collective-permute-done.6 = bf16[144,200]{1,0:T(8,128)(2,1)S(1)} collective-permute-done((bf16[144,200]{1,0:T(8,128)(2,1)S(1)}, bf16[144,200]{1,0:T(8,128)(2,1)S(1)}, u32[]{:S(2)}, u32[]{:S(2)}) %collective-permute-start.6) | collective-permute-done | bytes 57632 | tf_op jit(solution)/shard_map/ppermute | solution.py:307
  26.7 0.4 %collective-permute-done.5 = bf16[144,200]{1,0:T(8,128)(2,1)S(1)} collective-permute-done((bf16[144,200]{1,0:T(8,128)(2,1)S(1)}, bf16[144,200]{1,0:T(8,128)(2,1)S(1)}, u32[]{:S(2)}, u32[]{:S(2)}) %collective-permute-start.5) | collective-permute-done | bytes 57632 | tf_op jit(solution)/shard_map/ppermute | solution.py:307
  27.2 4.2 %collective-permute-start.7 = (f32[36,200]{1,0:T(8,128)S(1)}, f32[36,200]{1,0:T(8,128)S(1)}, u32[]{:S(2)}, u32[]{:S(2)}) collective-permute-start(f32[36,200]{1,0:T(8,128)S(1)} %get-tuple-element.26), channel_id=1, source_target_pairs={{0,24},{8,16},{16,8},{24,0},{1,25},{9,17},{17,9},{25,1},{2,26},{10... | collective-permute-start | bytes 86408 | tf_op jit(solution)/shard_map/ppermute | solution.py:313
  31.4 0.6 %collective-permute-start.8 = (f32[36,200]{1,0:T(8,128)S(1)}, f32[36,200]{1,0:T(8,128)S(1)}, u32[]{:S(2)}, u32[]{:S(2)}) collective-permute-start(f32[36,200]{1,0:T(8,128)S(1)} %get-tuple-element.28), channel_id=1, source_target_pairs={{0,16},{8,24},{16,0},{24,8},{1,17},{9,25},{17,1},{25,9},{2,18},{10... | collective-permute-start | bytes 86408 | tf_op jit(solution)/shard_map/ppermute | solution.py:313
  32.1 1.4 %collective-permute-done.7 = f32[36,200]{1,0:T(8,128)S(1)} collective-permute-done((f32[36,200]{1,0:T(8,128)S(1)}, f32[36,200]{1,0:T(8,128)S(1)}, u32[]{:S(2)}, u32[]{:S(2)}) %collective-permute-start.7) | collective-permute-done | bytes 28832 | tf_op jit(solution)/shard_map/ppermute | solution.py:313
  33.5 1.9 %collective-permute-done.9 = f32[36,200]{1,0:T(8,128)S(1)} collective-permute-done((f32[36,200]{1,0:T(8,128)S(1)}, f32[36,200]{1,0:T(8,128)S(1)}, u32[]{:S(2)}, u32[]{:S(2)}) %collective-permute-start.9) | collective-permute-done | bytes 28832 | tf_op jit(solution)/shard_map/ppermute | solution.py:313
  35.4 0.9 %collective-permute-done.8 = f32[36,200]{1,0:T(8,128)S(1)} collective-permute-done((f32[36,200]{1,0:T(8,128)S(1)}, f32[36,200]{1,0:T(8,128)S(1)}, u32[]{:S(2)}, u32[]{:S(2)}) %collective-permute-start.8) | collective-permute-done | bytes 28832 | tf_op jit(solution)/shard_map/ppermute | solution.py:313
  36.3 0.6 %fusion.5 = f32[200,36]{0,1:T(8,128)} fusion(f32[36,200]{1,0:T(8,128)S(1)} %collective-permute-done.9, f32[36,200]{1,0:T(8,128)S(1)} %collective-permute-done.8, f32[36,200]{1,0:T(8,128)S(1)} %collective-permute-done.7, f32[144,200]{1,0:T(8,128)S(1)} %fusion.2), kind=kLoop, calls=%fused_computation.10 | loop fusion | flops 21600 | bytes 144000 | tf_op jit(solution)/shard_map/transpose | solution.py:314
  (8 shorter events, 0.1 us)
Async XLA Ops:
  0.0 1.5 %copy-start = (bf16[3,16,32,384]{3,2,1,0:T(8,128)(2,1)S(1)}, bf16[3,16,32,384]{3,2,1,0:T(8,128)(2,1)}, u32[]{:S(2)}) copy-start(bf16[3,16,32,384]{3,2,1,0:T(8,128)(2,1)} %fields.1) | copy-start | bytes 3538948
  1.5 12.9 %collective-permute-start = (bf16[3,16,32,384]{3,2,1,0:T(8,128)(2,1)S(1)}, bf16[3,16,32,384]{3,2,1,0:T(8,128)(2,1)S(1)}, u32[]{:S(2)}, u32[]{:S(2)}) collective-permute-start(bf16[3,16,32,384]{3,2,1,0:T(8,128)(2,1)S(1)} %copy-done), channel_id=1, source_target_pairs={{0,1},{1,0},{2,3},{3,2},{4,5},{5,4},{6,7},{7,6},{8,9},{9,8},{10,11... | collective-permute-start | bytes 3538952 | tf_op jit(solution)/shard_map/ppermute | solution.py:294
  2.0 14.7 %collective-permute-start.1 = (bf16[2,8,32,384]{3,2,1,0:T(8,128)(2,1)S(1)}, bf16[2,8,32,384]{3,2,1,0:T(8,128)(2,1)S(1)}, u32[]{:S(2)}, u32[]{:S(2)}) collective-permute-start(bf16[2,8,32,384]{3,2,1,0:T(8,128)(2,1)S(1)} %pick.1), channel_id=1, source_target_pairs={{0,7},{1,2},{2,1},{3,4},{4,3},{5,6},{6,5},{7,0},{8,15},{9,10},{10,... | collective-permute-start | bytes 1179656 | tf_op jit(solution)/shard_map/ppermute | solution.py:293
  9.2 7.5 %collective-permute-start.2 = (bf16[32,1600]{1,0:T(8,128)(2,1)S(1)}, bf16[32,1600]{1,0:T(8,128)(2,1)S(1)}, u32[]{:S(2)}, u32[]{:S(2)}) collective-permute-start(bf16[32,1600]{1,0:T(8,128)(2,1)S(1)} %get-tuple-element.18), channel_id=1, source_target_pairs={{0,7},{1,2},{2,1},{3,4},{4,3},{5,6},{6,5},{7,0},{8,15},{9,10},{10,... | collective-permute-start | bytes 307208 | tf_op jit(solution)/shard_map/ppermute | solution.py:299
  17.5 2.1 %collective-permute-start.3 = (f32[4,144,200]{2,1,0:T(8,128)S(1)}, f32[4,144,200]{2,1,0:T(8,128)S(1)}, u32[]{:S(2)}, u32[]{:S(2)}) collective-permute-start(f32[4,144,200]{2,1,0:T(8,128)S(1)} %get-tuple-element.20), channel_id=1, source_target_pairs={{0,1},{1,0},{2,3},{3,2},{4,5},{5,4},{6,7},{7,6},{8,9},{9,8},{10,11... | collective-permute-start | bytes 1382408 | tf_op jit(solution)/shard_map/ppermute | solution.py:303
  19.7 5.5 %collective-permute-start.4 = (bf16[144,200]{1,0:T(8,128)(2,1)S(1)}, bf16[144,200]{1,0:T(8,128)(2,1)S(1)}, u32[]{:S(2)}, u32[]{:S(2)}) collective-permute-start(bf16[144,200]{1,0:T(8,128)(2,1)S(1)} %get-tuple-element.23), channel_id=1, source_target_pairs={{0,6},{1,7},{2,4},{3,5},{4,2},{5,3},{6,0},{7,1},{8,14},{9,15},{10,... | collective-permute-start | bytes 172808 | tf_op jit(solution)/shard_map/ppermute | solution.py:307
  22.4 4.4 %collective-permute-start.6 = (bf16[144,200]{1,0:T(8,128)(2,1)S(1)}, bf16[144,200]{1,0:T(8,128)(2,1)S(1)}, u32[]{:S(2)}, u32[]{:S(2)}) collective-permute-start(bf16[144,200]{1,0:T(8,128)(2,1)S(1)} %get-tuple-element.24), channel_id=1, source_target_pairs={{0,2},{1,3},{2,0},{3,1},{4,6},{5,7},{6,4},{7,5},{8,10},{9,11},{10,... | collective-permute-start | bytes 172808 | tf_op jit(solution)/shard_map/ppermute | solution.py:307
  22.8 4.4 %collective-permute-start.5 = (bf16[144,200]{1,0:T(8,128)(2,1)S(1)}, bf16[144,200]{1,0:T(8,128)(2,1)S(1)}, u32[]{:S(2)}, u32[]{:S(2)}) collective-permute-start(bf16[144,200]{1,0:T(8,128)(2,1)S(1)} %get-tuple-element.25), channel_id=1, source_target_pairs={{0,4},{1,5},{2,6},{3,7},{4,0},{5,1},{6,2},{7,3},{8,12},{9,13},{10,... | collective-permute-start | bytes 172808 | tf_op jit(solution)/shard_map/ppermute | solution.py:307
  27.2 6.3 %collective-permute-start.7 = (f32[36,200]{1,0:T(8,128)S(1)}, f32[36,200]{1,0:T(8,128)S(1)}, u32[]{:S(2)}, u32[]{:S(2)}) collective-permute-start(f32[36,200]{1,0:T(8,128)S(1)} %get-tuple-element.26), channel_id=1, source_target_pairs={{0,24},{8,16},{16,8},{24,0},{1,25},{9,17},{17,9},{25,1},{2,26},{10... | collective-permute-start | bytes 86408 | tf_op jit(solution)/shard_map/ppermute | solution.py:313
  31.4 4.0 %collective-permute-start.9 = (f32[36,200]{1,0:T(8,128)S(1)}, f32[36,200]{1,0:T(8,128)S(1)}, u32[]{:S(2)}, u32[]{:S(2)}) collective-permute-start(f32[36,200]{1,0:T(8,128)S(1)} %get-tuple-element.27), channel_id=1, source_target_pairs={{0,8},{8,0},{16,24},{24,16},{1,9},{9,1},{17,25},{25,17},{2,10},{10... | collective-permute-start | bytes 86408 | tf_op jit(solution)/shard_map/ppermute | solution.py:313
  31.4 4.9 %collective-permute-start.8 = (f32[36,200]{1,0:T(8,128)S(1)}, f32[36,200]{1,0:T(8,128)S(1)}, u32[]{:S(2)}, u32[]{:S(2)}) collective-permute-start(f32[36,200]{1,0:T(8,128)S(1)} %get-tuple-element.28), channel_id=1, source_target_pairs={{0,16},{8,24},{16,0},{24,8},{1,17},{9,25},{17,1},{25,9},{2,18},{10... | collective-permute-start | bytes 86408 | tf_op jit(solution)/shard_map/ppermute | solution.py:313

commit v4 on v3

--- a/solution.py
+++ b/solution.py
@@ -79,101 +79,6 @@
         compiler_params=grant(6),
         name="pick",
     )(requests, fields)
-
-
-def fold_kernel(
-    src_tiles, first, sends, requests, slots_ref, counts_ref, w_ref, e_ref, a_ref, *rest
-):
-    sent_ref, where, *totals = rest if sends else (None, *rest)
-    step = pl.program_id(0)
-    grids, tiles, depth, cells_x = w_ref.shape
-    slots = requests.shape[1]
-    cap = slots // 2
-    pairs = slots_ref.shape[1]
-    cells = depth // pairs
-    eofs = e_ref.shape[0]
-    lanes = a_ref.shape[2] // 2
-    chains = len(totals) // grids
-    _, lon, pair, _, base, _ = place()
-
-    @pl.when(step == 0)
-    def _():
-        for total in totals:
-            total[...] = jnp.zeros_like(total)
-        for g in range(grids):
-            ranks = [jnp.int32(0)] * 3
-            for r in range(slots):
-                owner = lax.div(requests[first + g, r, base + lon], src_tiles) - base
-                hits = [(owner == k).astype(jnp.int32) for k in (lon, pair)]
-                hits.append(1 - hits[0] - hits[1])
-                where[g, r] = sum(h * (k * cap + n) for k, (h, n) in enumerate(zip(hits, ranks)))
-                ranks = [n + h for n, h in zip(ranks, hits)]
-
-    for t in range(tiles):
-        tile = step * tiles + t
-        basis = e_ref[:, t * cells_x : (t + 1) * cells_x]
-        parts = [
-            lax.dot_general(
-                w_ref[g, t], basis, (((1,), (1,)), ((), ())), preferred_element_type=jnp.float32
-            )
-            for g in range(grids)
-        ]
-        for p in range(pairs):
-            for g in range(grids):
-                spot = where[g, slots_ref[first + g, p, tile]]
-                spot = jnp.where(p < counts_ref[first + g, tile], spot, 3 * cap)
-                rows = pl.ds(pl.multiple_of(spot * cells, cells), cells)
-                total = totals[g * chains + p % chains]
-                total[rows, :] += parts[g][p * cells : (p + 1) * cells]
-
-    @pl.when(step == pl.num_programs(0) - 1)
-    def _():
-        for g in range(grids):
-            own = totals[g * chains : (g + 1) * chains]
-            total = sum(part[: 3 * cap * cells, :] for part in own)
-            high = total.astype(jnp.bfloat16)
-            low = (total - high.astype(jnp.float32)).astype(jnp.bfloat16)
-            a_ref[g, :, :eofs] = high
-            a_ref[g, :, lanes : lanes + eofs] = low
-            if sends:
-                for j in range(cap):
-                    row = (2 * cap + j) * cells
-                    sent_ref[:, j * eofs : (j + 1) * eofs] = high[row : row + cells, :]
-
-
-def fold(requests, slots, counts, weights, eofs, src_tiles, first, grids, sends):
-    tile_total, depth, cells_x = weights.shape[1:]
-    cap = requests.shape[1] // 2
-    cells = depth // slots.shape[1]
-    lanes = pl.cdiv(eofs.shape[0], 128) * 128
-    tiles = tile_total // 2
-    chains = 2 if sends else 1
-    flops = 2 * grids * tile_total * depth * cells_x * eofs.shape[0]
-    shapes = [jax.ShapeDtypeStruct((grids, 3 * cap * cells, 2 * lanes), jnp.bfloat16)]
-    blocks = [pl.BlockSpec((grids, 3 * cap * cells, 2 * lanes), lambda i: (0, 0, 0))]
-    if sends:
-        shapes.append(jax.ShapeDtypeStruct((cells, cap * eofs.shape[0]), jnp.bfloat16))
-        blocks.append(pl.BlockSpec((cells, cap * eofs.shape[0]), lambda i: (0, 0)))
-    return pl.pallas_call(
-        functools.partial(fold_kernel, src_tiles, first, sends),
-        out_shape=shapes,
-        grid=(tile_total // tiles,),
-        in_specs=[
-            SMEM,
-            SMEM,
-            SMEM,
-            pl.BlockSpec((grids, tiles, depth, cells_x), lambda i: (first // grids, i, 0, 0)),
-            pl.BlockSpec((eofs.shape[0], tiles * cells_x), lambda i: (0, i)),
-        ],
-        out_specs=blocks,
-        scratch_shapes=[pltpu.SMEM((grids, 2 * cap), jnp.int32)]
-        + [pltpu.VMEM(((3 * cap + 1) * cells, eofs.shape[0]), jnp.float32)] * (grids * chains),
-        cost_estimate=pl.CostEstimate(
-            flops=8 * flops, bytes_accessed=grids * tile_total * depth * cells_x * 2, transcendentals=0
-        ),
-        compiler_params=grant(24),
-        name="fold",
-    )(requests, slots, counts, weights, eofs)
 
 
 def times(source, folded):
@@ -206,25 +111,117 @@
         kept_ref[j * cells : (j + 1) * cells, :] = fields[last, tile]
 
 
-def near(requests, fields, others, folded, last, eofs):
-    grids, _, cells, columns = fields.shape
+def fold_kernel(
+    src_tiles, first, sends, requests, slots_ref, counts_ref, w_ref, e_ref, *rest
+):
+    if sends:
+        a_ref, sent_ref, where, *totals = rest
+    else:
+        fields, others, last_ref, a_ref, near_ref, kept_ref, where, order, chosen, *totals = rest
+    step = pl.program_id(0)
+    grids, tiles, depth, cells_x = w_ref.shape
+    slots = requests.shape[1]
+    cap = slots // 2
+    pairs = slots_ref.shape[1]
+    cells = depth // pairs
+    eofs = e_ref.shape[0]
+    lanes = a_ref.shape[2] // 2
+    chains = len(totals) // grids
+    _, lon, pair, _, base, _ = place()
+
+    @pl.when(step == 0)
+    def _():
+        for total in totals:
+            total[...] = jnp.zeros_like(total)
+        for g in range(grids):
+            ranks = [jnp.int32(0)] * 3
+            for r in range(slots):
+                owner = lax.div(requests[first + g, r, base + lon], src_tiles) - base
+                hits = [(owner == k).astype(jnp.int32) for k in (lon, pair)]
+                hits.append(1 - hits[0] - hits[1])
+                where[g, r] = sum(h * (k * cap + n) for k, (h, n) in enumerate(zip(hits, ranks)))
+                ranks = [n + h for n, h in zip(ranks, hits)]
+
+    for t in range(tiles):
+        tile = step * tiles + t
+        basis = e_ref[:, t * cells_x : (t + 1) * cells_x]
+        parts = [
+            lax.dot_general(
+                w_ref[g, t], basis, (((1,), (1,)), ((), ())), preferred_element_type=jnp.float32
+            )
+            for g in range(grids)
+        ]
+        for p in range(pairs):
+            for g in range(grids):
+                spot = where[g, slots_ref[first + g, p, tile]]
+                spot = jnp.where(p < counts_ref[first + g, tile], spot, 3 * cap)
+                rows = pl.ds(pl.multiple_of(spot * cells, cells), cells)
+                total = totals[g * chains + p % chains]
+                total[rows, :] += parts[g][p * cells : (p + 1) * cells]
+
+    @pl.when(step == pl.num_programs(0) - 1)
+    def _():
+        for g in range(grids):
+            own = totals[g * chains : (g + 1) * chains]
+            total = sum(part[: 3 * cap * cells, :] for part in own)
+            high = total.astype(jnp.bfloat16)
+            low = (total - high.astype(jnp.float32)).astype(jnp.bfloat16)
+            a_ref[g, :, :eofs] = high
+            a_ref[g, :, lanes : lanes + eofs] = low
+            if sends:
+                for j in range(cap):
+                    row = (2 * cap + j) * cells
+                    sent_ref[:, j * eofs : (j + 1) * eofs] = high[row : row + cells, :]
+        if not sends:
+            near_kernel(
+                requests, fields, others, a_ref, last_ref, near_ref, kept_ref, order, chosen
+            )
+
+
+def fold(requests, slots, counts, weights, eofs, src_tiles, first, grids, chip=None):
+    sends = chip is None
+    tile_total, depth, cells_x = weights.shape[1:]
     cap = requests.shape[1] // 2
+    cells = depth // slots.shape[1]
+    lanes = pl.cdiv(eofs.shape[0], 128) * 128
+    tiles = tile_total // 2
+    chains = 2 if sends else 1
+    flops = 2 * grids * tile_total * depth * cells_x * eofs.shape[0]
+    shapes = [jax.ShapeDtypeStruct((grids, 3 * cap * cells, 2 * lanes), jnp.bfloat16)]
+    blocks = [pl.BlockSpec((grids, 3 * cap * cells, 2 * lanes), lambda i: (0, 0, 0))]
+    if sends:
+        shapes.append(jax.ShapeDtypeStruct((cells, cap * eofs.shape[0]), jnp.bfloat16))
+        blocks.append(pl.BlockSpec((cells, cap * eofs.shape[0]), lambda i: (0, 0)))
+    held = [pltpu.SMEM((grids, 2 * cap), jnp.int32)]
+    if not sends:
+        fields = chip[0]
+        columns = fields.shape[3]
+        shapes.append(jax.ShapeDtypeStruct((fields.shape[0] * columns, eofs.shape[0]), jnp.float32))
+        shapes.append(jax.ShapeDtypeStruct((cap * cells, columns), fields.dtype))
+        blocks += [VMEM, VMEM]
+        held.append(pltpu.SMEM((cap + 1,), jnp.int32))
+        held.append(pltpu.VMEM((2 * cap * cells, columns), fields.dtype))
     return pl.pallas_call(
-        near_kernel,
-        out_shape=(
-            jax.ShapeDtypeStruct((grids * columns, eofs), jnp.float32),
-            jax.ShapeDtypeStruct((cap * cells, columns), fields.dtype),
+        functools.partial(fold_kernel, src_tiles, first, sends),
+        out_shape=shapes,
+        grid=(tile_total // tiles,),
+        in_specs=[
+            SMEM,
+            SMEM,
+            SMEM,
+            pl.BlockSpec((grids, tiles, depth, cells_x), lambda i: (first // grids, i, 0, 0)),
+            pl.BlockSpec((eofs.shape[0], tiles * cells_x), lambda i: (0, i)),
+        ]
+        + [VMEM] * len(chip or ()),
+        out_specs=blocks,
+        scratch_shapes=held
+        + [pltpu.VMEM(((3 * cap + 1) * cells, eofs.shape[0]), jnp.float32)] * (grids * chains),
+        cost_estimate=pl.CostEstimate(
+            flops=8 * flops, bytes_accessed=grids * tile_total * depth * cells_x * 2, transcendentals=0
         ),
-        in_specs=[SMEM, VMEM, VMEM, VMEM, VMEM],
-        out_specs=(VMEM, VMEM),
-        scratch_shapes=[
-            pltpu.SMEM((cap + 1,), jnp.int32),
-            pltpu.VMEM((2 * cap * cells, columns), fields.dtype),
-        ],
-        cost_estimate=pl.CostEstimate(flops=10**9, bytes_accessed=10**6, transcendentals=0),
-        compiler_params=grant(12),
-        name="near",
-    )(requests, fields, others, folded, last)
+        compiler_params=grant(24 if sends else 32),
+        name="fold",
+    )(requests, slots, counts, weights, eofs, *(chip or ()))
 
 
 def far_kernel(
@@ -295,10 +292,9 @@
     grids, tile_total, pairs, cells, cells_x = weights.shape
     weights = stay(weights.reshape(grids, tile_total, pairs * cells, cells_x))
     tables = (requests, pair_slots, pair_counts, weights, eofs, fields.shape[1])
-    last, spread = fold(*tables, grids - 1, 1, True)
+    last, spread = fold(*tables, grids - 1, 1)
     spread = lax.ppermute(spread, "lon", off_chip)
-    (folded,) = fold(*tables, 0, grids - 1, False)
-    near_part, kept = near(requests, fields, others, folded, last, eofs.shape[0])
+    folded, near_part, kept = fold(*tables, 0, grids - 1, (fields, others, last))
     keep, send = far(near_part, tiles, kept, folded, spread)
     pair_sum = keep + lax.ppermute(send, "lon", on_chip)
     plane_sum = pair_sum[0]

time: 37.2 us -> 37.1 us (level)
  Pallas kernels: 13.1 us -> 11.8 us
  waiting for transfers between devices: 10.1 us -> 11.3 us
    pallas_call x1 -> x0, Pallas kernels: 2.34 us -> none  [near(): pl.pallas_call(near_kernel, out_shape=(jax.ShapeDtypeStruct((grids * colu...]
    ppermute x1, waiting for transfers between devices: 0.01 us -> 1.22 us  [shards(): spread = lax.ppermute(spread, 'lon', off_chip)]
    pallas_call x2, Pallas kernels: 8.72 us -> 9.8 us  [fold(): pl.pallas_call(functools.partial(fold_kernel, src_tiles, first, sends), o...]
  transfers between devices with their start and end apart: 10 -> 10, of which waited for: 7 -> 8; matrix products, arithmetic and copies ran while one was open for 0% -> 0% of each run, Pallas kernels for 30% -> 27%
where the time goes in v4:
time: 37.1 us; the launch traced here: 36.9 us
  starting transfers between devices  12.7 us (34%)
  Pallas kernels  11.8 us (32%)
  waiting for transfers between devices  11.3 us (30%)
  other arithmetic  0.79 us (2%)
    pallas_call x2, Pallas kernels, fold(): pl.pallas_call(functools.partial(fold_kernel, src_tiles, first, sends), o...  9.8 us
    ppermute x3, starting transfers between devices, shards(): lax.ppermute(plane_sum[q * rows:(q + 1) * rows], 'lat', swap)  4.95 us
    ppermute x3, waiting for transfers between devices, shards(): lax.ppermute(plane_sum[q * rows:(q + 1) * rows], 'lat', swap)  4.26 us
    ppermute x3, waiting for transfers between devices, shards(): sent = lax.ppermute(pair_sum[r].astype(jnp.bfloat16), 'lon', swap)  3.85 us
    ppermute x3, starting transfers between devices, shards(): sent = lax.ppermute(pair_sum[r].astype(jnp.bfloat16), 'lon', swap)  3.55 us
    ppermute x1, starting transfers between devices, shards(): tiles = lax.ppermute(picked, 'lon', off_chip)  3.54 us
    ppermute x1, waiting for transfers between devices, shards(): pair_sum = keep + lax.ppermute(send, 'lon', on_chip)  1.99 us
    pallas_call x1, Pallas kernels, pick(): pl.pallas_call(pick_kernel, out_shape=jax.ShapeDtypeStruct((grids, cap, c...  1.25 us
  transfers between devices with their start and end apart: 10, of which 8 were waited for; matrix products, arithmetic and copies ran while one was open for 0% of the time, Pallas kernels for 27%

profile of v4, /device:TPU:0, one launch (start us, length us, event | category | flops | bytes accessed | tf_op | source)
XLA Modules:
  0.0 36.9 jit_solution(16354722844111658305)
XLA Ops:
  0.0 1.3 %pick.1 = bf16[2,8,32,384]{3,2,1,0:T(8,128)(2,1)S(1)} custom-call(s32[3,16,32]{2,1,0:T(8,128)} %bitcast.19, bf16[3,16,32,384]{3,2,1,0:T(8,128)(2,1)} %rest_0_.1), custom_call_target="tpu_custom_call" | custom-call | tf_op jit(solution)/shard_map/pick/pallas_call | solution.py:68
  1.3 0.2 copy-done
  1.5 0.5 %collective-permute-start = (bf16[3,16,32,384]{3,2,1,0:T(8,128)(2,1)S(1)}, bf16[3,16,32,384]{3,2,1,0:T(8,128)(2,1)S(1)}, u32[]{:S(2)}, u32[]{:S(2)}) collective-permute-start(bf16[3,16,32,384]{3,2,1,0:T(8,128)(2,1)S(1)} %copy-done), channel_id=1, source_target_pairs={{0,1},{1,0},{2,3},{3,2},{4,5},{5,4},{6,7},{7,6},{8,9},{9,8},{10,11... | collective-permute-start | bytes 3538952 | tf_op jit(solution)/shard_map/ppermute | solution.py:291
  2.0 3.5 %collective-permute-start.1 = (bf16[2,8,32,384]{3,2,1,0:T(8,128)(2,1)S(1)}, bf16[2,8,32,384]{3,2,1,0:T(8,128)(2,1)S(1)}, u32[]{:S(2)}, u32[]{:S(2)}) collective-permute-start(bf16[2,8,32,384]{3,2,1,0:T(8,128)(2,1)S(1)} %pick.1), channel_id=1, source_target_pairs={{0,7},{1,2},{2,1},{3,4},{4,3},{5,6},{6,5},{7,0},{8,15},{9,10},{10,... | collective-permute-start | bytes 1179656 | tf_op jit(solution)/shard_map/ppermute | solution.py:290
  5.5 3.6 %fold.2 = (bf16[1,768,512]{2,1,0:T(8,128)(2,1)S(1)}, bf16[32,1600]{1,0:T(8,128)(2,1)S(1)}) custom-call(s32[3,16,32]{2,1,0:T(8,128)} %bitcast.20, s32[3,8,32]{2,1,0:T(8,128)} %bitcast.24, s32[3,32]{1,0:T(4,128)} %counts_ref.3, bf16[3,32,256,128]{3,2,1,0:T(8,128)(2,1)} %bitcast.22, bf16[200,4096]{1,0:T(8,128)(2,1)} %e_ref.3), custom_call_target="tpu_custom_call" | custom-call | flops 3355443200 | bytes 2097152 | tf_op jit(solution)/shard_map/fold/pallas_call | solution.py:204
  9.2 0.1 collective-permute-start.2
  9.3 6.2 %fold.3 = (bf16[2,768,512]{2,1,0:T(8,128)(2,1)S(1)}, f32[1152,200]{1,0:T(8,128)S(1)}, bf16[256,384]{1,0:T(8,128)(2,1)S(1)}) custom-call(s32[3,16,32]{2,1,0:T(8,128)} %bitcast.21, s32[3,8,32]{2,1,0:T(8,128)} %bitcast.25, s32[3,32]{1,0:T(4,128)} %counts_ref.3, bf16[3,32,256,128]{3,2,1,0:T(8,128)(2,1)} %bitcast.23, bf16[200,4096]{1,0:T(8,128)(2,1)} %e_ref.3, ...), custom_call_target="tpu_custom_call" | custom-call | flops 6710886400 | bytes 4194304 | tf_op jit(solution)/shard_map/fold/pallas_call | solution.py:204
  15.5 1.2 %collective-permute-done.2.others_ref = bf16[32,1600]{1,0:T(8,128)(2,1)S(1)} collective-permute-done((bf16[32,1600]{1,0:T(8,128)(2,1)S(1)}, bf16[32,1600]{1,0:T(8,128)(2,1)S(1)}, u32[]{:S(2)}, u32[]{:S(2)}) %collective-permute-start.2) | collective-permute-done | bytes 102432 | tf_op jit(solution)/shard_map/ppermute | solution.py:296
  16.7 0.7 %far.1 = (f32[4,144,200]{2,1,0:T(8,128)S(1)}, f32[4,144,200]{2,1,0:T(8,128)S(1)}) custom-call(f32[1152,200]{1,0:T(8,128)S(1)} %get-tuple-element.16.near_ref, bf16[2,8,32,384]{3,2,1,0:T(8,128)(2,1)S(1)} %collective-permute-done.1.tiles, bf16[256,384]{1,0:T(8,128)(2,1)S(1)} %get-tuple-element.18.kept, bf16[2,768,512]{2,1,0:T(8,128)(2,1)S(1)} %get-tuple-element.19.a_ref, ...), custom_call_target="tpu_custom_call" | custom-call | tf_op jit(solution)/shard_map/far/pallas_call | solution.py:265
  17.4 0.1 collective-permute-start.3
  17.5 2.0 %collective-permute-done.3 = f32[4,144,200]{2,1,0:T(8,128)S(1)} collective-permute-done((f32[4,144,200]{2,1,0:T(8,128)S(1)}, f32[4,144,200]{2,1,0:T(8,128)S(1)}, u32[]{:S(2)}, u32[]{:S(2)}) %collective-permute-start.3) | collective-permute-done | bytes 460832 | tf_op jit(solution)/shard_map/ppermute | solution.py:299
  19.5 0.1 fusion.6
  19.6 1.9 %collective-permute-start.4 = (bf16[144,200]{1,0:T(8,128)(2,1)S(1)}, bf16[144,200]{1,0:T(8,128)(2,1)S(1)}, u32[]{:S(2)}, u32[]{:S(2)}) collective-permute-start(bf16[144,200]{1,0:T(8,128)(2,1)S(1)} %get-tuple-element.25), channel_id=1, source_target_pairs={{0,6},{1,7},{2,4},{3,5},{4,2},{5,3},{6,0},{7,1},{8,14},{9,15},{10,... | collective-permute-start | bytes 172808 | tf_op jit(solution)/shard_map/ppermute | solution.py:303
  21.6 1.1 %collective-permute-start.6 = (bf16[144,200]{1,0:T(8,128)(2,1)S(1)}, bf16[144,200]{1,0:T(8,128)(2,1)S(1)}, u32[]{:S(2)}, u32[]{:S(2)}) collective-permute-start(bf16[144,200]{1,0:T(8,128)(2,1)S(1)} %get-tuple-element.26), channel_id=1, source_target_pairs={{0,2},{1,3},{2,0},{3,1},{4,6},{5,7},{6,4},{7,5},{8,10},{9,11},{10,... | collective-permute-start | bytes 172808 | tf_op jit(solution)/shard_map/ppermute | solution.py:303
  22.7 0.5 %collective-permute-start.5 = (bf16[144,200]{1,0:T(8,128)(2,1)S(1)}, bf16[144,200]{1,0:T(8,128)(2,1)S(1)}, u32[]{:S(2)}, u32[]{:S(2)}) collective-permute-start(bf16[144,200]{1,0:T(8,128)(2,1)S(1)} %get-tuple-element.27), channel_id=1, source_target_pairs={{0,4},{1,5},{2,6},{3,7},{4,0},{5,1},{6,2},{7,3},{8,12},{9,13},{10,... | collective-permute-start | bytes 172808 | tf_op jit(solution)/shard_map/ppermute | solution.py:303
  23.2 1.8 %collective-permute-done.4 = bf16[144,200]{1,0:T(8,128)(2,1)S(1)} collective-permute-done((bf16[144,200]{1,0:T(8,128)(2,1)S(1)}, bf16[144,200]{1,0:T(8,128)(2,1)S(1)}, u32[]{:S(2)}, u32[]{:S(2)}) %collective-permute-start.4) | collective-permute-done | bytes 57632 | tf_op jit(solution)/shard_map/ppermute | solution.py:303
  25.0 1.6 %collective-permute-done.6 = bf16[144,200]{1,0:T(8,128)(2,1)S(1)} collective-permute-done((bf16[144,200]{1,0:T(8,128)(2,1)S(1)}, bf16[144,200]{1,0:T(8,128)(2,1)S(1)}, u32[]{:S(2)}, u32[]{:S(2)}) %collective-permute-start.6) | collective-permute-done | bytes 57632 | tf_op jit(solution)/shard_map/ppermute | solution.py:303
  26.6 0.4 %collective-permute-done.5 = bf16[144,200]{1,0:T(8,128)(2,1)S(1)} collective-permute-done((bf16[144,200]{1,0:T(8,128)(2,1)S(1)}, bf16[144,200]{1,0:T(8,128)(2,1)S(1)}, u32[]{:S(2)}, u32[]{:S(2)}) %collective-permute-start.5) | collective-permute-done | bytes 57632 | tf_op jit(solution)/shard_map/ppermute | solution.py:303
  27.1 4.3 %collective-permute-start.7 = (f32[36,200]{1,0:T(8,128)S(1)}, f32[36,200]{1,0:T(8,128)S(1)}, u32[]{:S(2)}, u32[]{:S(2)}) collective-permute-start(f32[36,200]{1,0:T(8,128)S(1)} %get-tuple-element.28), channel_id=1, source_target_pairs={{0,24},{8,16},{16,8},{24,0},{1,25},{9,17},{17,9},{25,1},{2,26},{10... | collective-permute-start | bytes 86408 | tf_op jit(solution)/shard_map/ppermute | solution.py:309
  31.4 0.6 %collective-permute-start.8 = (f32[36,200]{1,0:T(8,128)S(1)}, f32[36,200]{1,0:T(8,128)S(1)}, u32[]{:S(2)}, u32[]{:S(2)}) collective-permute-start(f32[36,200]{1,0:T(8,128)S(1)} %get-tuple-element.30), channel_id=1, source_target_pairs={{0,16},{8,24},{16,0},{24,8},{1,17},{9,25},{17,1},{25,9},{2,18},{10... | collective-permute-start | bytes 86408 | tf_op jit(solution)/shard_map/ppermute | solution.py:309
  32.1 1.4 %collective-permute-done.7 = f32[36,200]{1,0:T(8,128)S(1)} collective-permute-done((f32[36,200]{1,0:T(8,128)S(1)}, f32[36,200]{1,0:T(8,128)S(1)}, u32[]{:S(2)}, u32[]{:S(2)}) %collective-permute-start.7) | collective-permute-done | bytes 28832 | tf_op jit(solution)/shard_map/ppermute | solution.py:309
  33.4 2.0 %collective-permute-done.9 = f32[36,200]{1,0:T(8,128)S(1)} collective-permute-done((f32[36,200]{1,0:T(8,128)S(1)}, f32[36,200]{1,0:T(8,128)S(1)}, u32[]{:S(2)}, u32[]{:S(2)}) %collective-permute-start.9) | collective-permute-done | bytes 28832 | tf_op jit(solution)/shard_map/ppermute | solution.py:309
  35.4 0.9 %collective-permute-done.8 = f32[36,200]{1,0:T(8,128)S(1)} collective-permute-done((f32[36,200]{1,0:T(8,128)S(1)}, f32[36,200]{1,0:T(8,128)S(1)}, u32[]{:S(2)}, u32[]{:S(2)}) %collective-permute-start.8) | collective-permute-done | bytes 28832 | tf_op jit(solution)/shard_map/ppermute | solution.py:309
  36.3 0.6 %fusion.5 = f32[200,36]{0,1:T(8,128)} fusion(f32[36,200]{1,0:T(8,128)S(1)} %collective-permute-done.9, f32[36,200]{1,0:T(8,128)S(1)} %collective-permute-done.8, f32[36,200]{1,0:T(8,128)S(1)} %collective-permute-done.7, f32[144,200]{1,0:T(8,128)S(1)} %fusion.2), kind=kLoop, calls=%fused_computation.10 | loop fusion | flops 21600 | bytes 144000 | tf_op jit(solution)/shard_map/transpose | solution.py:310
  (7 shorter events, 0.1 us)
Async XLA Ops:
  0.0 1.5 %copy-start = (bf16[3,16,32,384]{3,2,1,0:T(8,128)(2,1)S(1)}, bf16[3,16,32,384]{3,2,1,0:T(8,128)(2,1)}, u32[]{:S(2)}) copy-start(bf16[3,16,32,384]{3,2,1,0:T(8,128)(2,1)} %rest_0_.1) | copy-start | bytes 3538948
  1.5 7.8 %collective-permute-start = (bf16[3,16,32,384]{3,2,1,0:T(8,128)(2,1)S(1)}, bf16[3,16,32,384]{3,2,1,0:T(8,128)(2,1)S(1)}, u32[]{:S(2)}, u32[]{:S(2)}) collective-permute-start(bf16[3,16,32,384]{3,2,1,0:T(8,128)(2,1)S(1)} %copy-done), channel_id=1, source_target_pairs={{0,1},{1,0},{2,3},{3,2},{4,5},{5,4},{6,7},{7,6},{8,9},{9,8},{10,11... | collective-permute-start | bytes 3538952 | tf_op jit(solution)/shard_map/ppermute | solution.py:291
  2.0 14.7 %collective-permute-start.1 = (bf16[2,8,32,384]{3,2,1,0:T(8,128)(2,1)S(1)}, bf16[2,8,32,384]{3,2,1,0:T(8,128)(2,1)S(1)}, u32[]{:S(2)}, u32[]{:S(2)}) collective-permute-start(bf16[2,8,32,384]{3,2,1,0:T(8,128)(2,1)S(1)} %pick.1), channel_id=1, source_target_pairs={{0,7},{1,2},{2,1},{3,4},{4,3},{5,6},{6,5},{7,0},{8,15},{9,10},{10,... | collective-permute-start | bytes 1179656 | tf_op jit(solution)/shard_map/ppermute | solution.py:290
  9.2 7.5 %collective-permute-start.2 = (bf16[32,1600]{1,0:T(8,128)(2,1)S(1)}, bf16[32,1600]{1,0:T(8,128)(2,1)S(1)}, u32[]{:S(2)}, u32[]{:S(2)}) collective-permute-start(bf16[32,1600]{1,0:T(8,128)(2,1)S(1)} %get-tuple-element.20), channel_id=1, source_target_pairs={{0,7},{1,2},{2,1},{3,4},{4,3},{5,6},{6,5},{7,0},{8,15},{9,10},{10,... | collective-permute-start | bytes 307208 | tf_op jit(solution)/shard_map/ppermute | solution.py:296
  17.4 2.1 %collective-permute-start.3 = (f32[4,144,200]{2,1,0:T(8,128)S(1)}, f32[4,144,200]{2,1,0:T(8,128)S(1)}, u32[]{:S(2)}, u32[]{:S(2)}) collective-permute-start(f32[4,144,200]{2,1,0:T(8,128)S(1)} %get-tuple-element.22), channel_id=1, source_target_pairs={{0,1},{1,0},{2,3},{3,2},{4,5},{5,4},{6,7},{7,6},{8,9},{9,8},{10,11... | collective-permute-start | bytes 1382408 | tf_op jit(solution)/shard_map/ppermute | solution.py:299
  19.6 5.3 %collective-permute-start.4 = (bf16[144,200]{1,0:T(8,128)(2,1)S(1)}, bf16[144,200]{1,0:T(8,128)(2,1)S(1)}, u32[]{:S(2)}, u32[]{:S(2)}) collective-permute-start(bf16[144,200]{1,0:T(8,128)(2,1)S(1)} %get-tuple-element.25), channel_id=1, source_target_pairs={{0,6},{1,7},{2,4},{3,5},{4,2},{5,3},{6,0},{7,1},{8,14},{9,15},{10,... | collective-permute-start | bytes 172808 | tf_op jit(solution)/shard_map/ppermute | solution.py:303
  21.6 5.0 %collective-permute-start.6 = (bf16[144,200]{1,0:T(8,128)(2,1)S(1)}, bf16[144,200]{1,0:T(8,128)(2,1)S(1)}, u32[]{:S(2)}, u32[]{:S(2)}) collective-permute-start(bf16[144,200]{1,0:T(8,128)(2,1)S(1)} %get-tuple-element.26), channel_id=1, source_target_pairs={{0,2},{1,3},{2,0},{3,1},{4,6},{5,7},{6,4},{7,5},{8,10},{9,11},{10,... | collective-permute-start | bytes 172808 | tf_op jit(solution)/shard_map/ppermute | solution.py:303
  22.7 4.4 %collective-permute-start.5 = (bf16[144,200]{1,0:T(8,128)(2,1)S(1)}, bf16[144,200]{1,0:T(8,128)(2,1)S(1)}, u32[]{:S(2)}, u32[]{:S(2)}) collective-permute-start(bf16[144,200]{1,0:T(8,128)(2,1)S(1)} %get-tuple-element.27), channel_id=1, source_target_pairs={{0,4},{1,5},{2,6},{3,7},{4,0},{5,1},{6,2},{7,3},{8,12},{9,13},{10,... | collective-permute-start | bytes 172808 | tf_op jit(solution)/shard_map/ppermute | solution.py:303
  27.1 6.3 %collective-permute-start.7 = (f32[36,200]{1,0:T(8,128)S(1)}, f32[36,200]{1,0:T(8,128)S(1)}, u32[]{:S(2)}, u32[]{:S(2)}) collective-permute-start(f32[36,200]{1,0:T(8,128)S(1)} %get-tuple-element.28), channel_id=1, source_target_pairs={{0,24},{8,16},{16,8},{24,0},{1,25},{9,17},{17,9},{25,1},{2,26},{10... | collective-permute-start | bytes 86408 | tf_op jit(solution)/shard_map/ppermute | solution.py:309
  31.4 4.0 %collective-permute-start.9 = (f32[36,200]{1,0:T(8,128)S(1)}, f32[36,200]{1,0:T(8,128)S(1)}, u32[]{:S(2)}, u32[]{:S(2)}) collective-permute-start(f32[36,200]{1,0:T(8,128)S(1)} %get-tuple-element.29), channel_id=1, source_target_pairs={{0,8},{8,0},{16,24},{24,16},{1,9},{9,1},{17,25},{25,17},{2,10},{10... | collective-permute-start | bytes 86408 | tf_op jit(solution)/shard_map/ppermute | solution.py:309
  31.4 4.9 %collective-permute-start.8 = (f32[36,200]{1,0:T(8,128)S(1)}, f32[36,200]{1,0:T(8,128)S(1)}, u32[]{:S(2)}, u32[]{:S(2)}) collective-permute-start(f32[36,200]{1,0:T(8,128)S(1)} %get-tuple-element.30), channel_id=1, source_target_pairs={{0,16},{8,24},{16,0},{24,8},{1,17},{9,25},{17,1},{25,9},{2,18},{10... | collective-permute-start | bytes 86408 | tf_op jit(solution)/shard_map/ppermute | solution.py:309

commit v5 on v4

--- a/solution.py
+++ b/solution.py
@@ -10,6 +10,7 @@
 
 MONTHS = 24
 CORES = 2
+SIDE = 3
 MIB = 2**20
 
 SMEM = pl.BlockSpec(memory_space=pltpu.SMEM)
@@ -233,6 +234,8 @@
     lanes = a_ref.shape[2] // 2
     planes = lon_count // CORES
     rows = units.shape[1]
+    part_rows = keep_ref.shape[1] // lat_count
+    side = rows // part_rows
     for g in range(grids):
         part = slice(g * columns, (g + 1) * columns)
         if g < grids - 1:
@@ -254,14 +257,18 @@
             for q in range(lat_count):
                 target = jnp.bitwise_xor(lat, q) * lon_count
                 target += jnp.bitwise_xor(plane, r) * CORES + jnp.bitwise_xor(core, c)
-                out[r, q * rows : (q + 1) * rows, :] = units[target]
+                for i in range(side):
+                    piece = units[target, i * part_rows : (i + 1) * part_rows, :]
+                    out[r, q * part_rows : (q + 1) * part_rows, i * eofs : (i + 1) * eofs] = piece
 
 
 def far(near_part, tiles, kept, folded, others):
     lat_count, lon_count = lax.axis_size("lat"), lax.axis_size("lon")
     total_columns, eofs = near_part.shape
     rows = total_columns // (lat_count * lon_count)
-    block = jax.ShapeDtypeStruct((lon_count // CORES, lat_count * rows, eofs), jnp.float32)
+    side = SIDE if rows % SIDE == 0 else 1
+    shape = (lon_count // CORES, lat_count * rows // side, side * eofs)
+    block = jax.ShapeDtypeStruct(shape, jnp.float32)
     return pl.pallas_call(
         functools.partial(far_kernel, lat_count),
         out_shape=(block, block),
@@ -275,6 +282,26 @@
         compiler_params=grant(16),
         name="far",
     )(near_part, tiles, kept, folded, others)
+
+
+def finish_kernel(*refs):
+    *parts, out_ref = refs
+    total = sum(part[...] for part in parts)
+    rows, eofs = parts[0].shape[0], out_ref.shape[1]
+    for i in range(out_ref.shape[0] // rows):
+        out_ref[i * rows : (i + 1) * rows, :] = total[:, i * eofs : (i + 1) * eofs]
+
+
+def finish(parts, eofs):
+    size = parts[0].size // eofs
+    return pl.pallas_call(
+        finish_kernel,
+        out_shape=jax.ShapeDtypeStruct((size, eofs), jnp.float32),
+        in_specs=[VMEM] * len(parts),
+        out_specs=VMEM,
+        compiler_params=grant(2),
+        name="finish",
+    )(*parts)
 
 
 def shards(fields, weights, pair_slots, pair_counts, requests, eofs):
@@ -303,11 +330,11 @@
         sent = lax.ppermute(pair_sum[r].astype(jnp.bfloat16), "lon", swap)
         plane_sum = plane_sum + sent.astype(jnp.float32)
     rows = plane_sum.shape[0] // lat_count
-    total = plane_sum[:rows]
+    parts = [plane_sum[:rows]]
     for q in reversed(range(1, lat_count)):
         swap = [(i, i ^ q) for i in range(lat_count)]
-        total = total + lax.ppermute(plane_sum[q * rows : (q + 1) * rows], "lat", swap)
-    return total.T
+        parts.append(lax.ppermute(plane_sum[q * rows : (q + 1) * rows], "lat", swap))
+    return finish(parts, eofs.shape[0]).T
 
 
 def solution(mesh):

time: 37.1 us -> 38.6 us (1.040)
  waiting for transfers between devices: 11.3 us -> 12.6 us
  Pallas kernels: 11.8 us -> 12.8 us
  other arithmetic: 0.79 us -> 0.14 us
    ppermute x3, waiting for transfers between devices: 4.26 us -> 5.8 us  [shards(): parts.append(lax.ppermute(plane_sum[q * rows:(q + 1) * rows], 'lat', swap))]
    pallas_call x0 -> x1, Pallas kernels: none -> 0.7 us  [finish(): pl.pallas_call(finish_kernel, out_shape=jax.ShapeDtypeStruct((size, eofs)...]
    transpose x1 -> x0, other arithmetic: 0.63 us -> none  [shards(): return total.T]
  transfers between devices with their start and end apart: 10 -> 10, of which waited for: 8 -> 7; matrix products, arithmetic and copies ran while one was open for 0% -> 0% of each run, Pallas kernels for 27% -> 26%
where the time goes in v5:
time: 38.6 us; the launch traced here: 38.4 us
  Pallas kernels  12.8 us (33%)
  starting transfers between devices  12.6 us (33%)
  waiting for transfers between devices  12.6 us (33%)
    pallas_call x2, Pallas kernels, fold(): pl.pallas_call(functools.partial(fold_kernel, src_tiles, first, sends), o...  9.8 us
    ppermute x3, waiting for transfers between devices, shards(): parts.append(lax.ppermute(plane_sum[q * rows:(q + 1) * rows], 'lat', swap))  5.8 us
    ppermute x3, starting transfers between devices, shards(): parts.append(lax.ppermute(plane_sum[q * rows:(q + 1) * rows], 'lat', swap))  4.88 us
    ppermute x3, waiting for transfers between devices, shards(): sent = lax.ppermute(pair_sum[r].astype(jnp.bfloat16), 'lon', swap)  3.71 us
    ppermute x3, starting transfers between devices, shards(): sent = lax.ppermute(pair_sum[r].astype(jnp.bfloat16), 'lon', swap)  3.55 us
    ppermute x1, starting transfers between devices, shards(): tiles = lax.ppermute(picked, 'lon', off_chip)  3.54 us
    ppermute x1, waiting for transfers between devices, shards(): pair_sum = keep + lax.ppermute(send, 'lon', on_chip)  1.85 us
    pallas_call x1, Pallas kernels, pick(): pl.pallas_call(pick_kernel, out_shape=jax.ShapeDtypeStruct((grids, cap, c...  1.25 us
  transfers between devices with their start and end apart: 10, of which 7 were waited for; matrix products, arithmetic and copies ran while one was open for 0% of the time, Pallas kernels for 26%

profile of v5, /device:TPU:0, one launch (start us, length us, event | category | flops | bytes accessed | tf_op | source)
XLA Modules:
  0.0 38.4 jit_solution(16353346733970604301)
XLA Ops:
  0.0 1.3 %pick.1 = bf16[2,8,32,384]{3,2,1,0:T(8,128)(2,1)S(1)} custom-call(s32[3,16,32]{2,1,0:T(8,128)} %bitcast.18, bf16[3,16,32,384]{3,2,1,0:T(8,128)(2,1)} %rest_0_.1), custom_call_target="tpu_custom_call" | custom-call | tf_op jit(solution)/shard_map/pick/pallas_call | solution.py:69
  1.3 0.2 copy-done
  1.5 0.5 %collective-permute-start = (bf16[3,16,32,384]{3,2,1,0:T(8,128)(2,1)S(1)}, bf16[3,16,32,384]{3,2,1,0:T(8,128)(2,1)S(1)}, u32[]{:S(2)}, u32[]{:S(2)}) collective-permute-start(bf16[3,16,32,384]{3,2,1,0:T(8,128)(2,1)S(1)} %copy-done), channel_id=1, source_target_pairs={{0,1},{1,0},{2,3},{3,2},{4,5},{5,4},{6,7},{7,6},{8,9},{9,8},{10,11... | collective-permute-start | bytes 3538952 | tf_op jit(solution)/shard_map/ppermute | solution.py:318
  2.0 3.5 %collective-permute-start.1 = (bf16[2,8,32,384]{3,2,1,0:T(8,128)(2,1)S(1)}, bf16[2,8,32,384]{3,2,1,0:T(8,128)(2,1)S(1)}, u32[]{:S(2)}, u32[]{:S(2)}) collective-permute-start(bf16[2,8,32,384]{3,2,1,0:T(8,128)(2,1)S(1)} %pick.1), channel_id=1, source_target_pairs={{0,7},{1,2},{2,1},{3,4},{4,3},{5,6},{6,5},{7,0},{8,15},{9,10},{10,... | collective-permute-start | bytes 1179656 | tf_op jit(solution)/shard_map/ppermute | solution.py:317
  5.5 3.6 %fold.2 = (bf16[1,768,512]{2,1,0:T(8,128)(2,1)S(1)}, bf16[32,1600]{1,0:T(8,128)(2,1)S(1)}) custom-call(s32[3,16,32]{2,1,0:T(8,128)} %bitcast.19, s32[3,8,32]{2,1,0:T(8,128)} %bitcast.23, s32[3,32]{1,0:T(4,128)} %counts_ref.3, bf16[3,32,256,128]{3,2,1,0:T(8,128)(2,1)} %bitcast.21, bf16[200,4096]{1,0:T(8,128)(2,1)} %e_ref.3), custom_call_target="tpu_custom_call" | custom-call | flops 3355443200 | bytes 2097152 | tf_op jit(solution)/shard_map/fold/pallas_call | solution.py:205
  9.2 0.1 collective-permute-start.2
  9.3 0.0 collective-permute-done.rest_1_
  9.3 6.2 %fold.3 = (bf16[2,768,512]{2,1,0:T(8,128)(2,1)S(1)}, f32[1152,200]{1,0:T(8,128)S(1)}, bf16[256,384]{1,0:T(8,128)(2,1)S(1)}) custom-call(s32[3,16,32]{2,1,0:T(8,128)} %bitcast.20, s32[3,8,32]{2,1,0:T(8,128)} %bitcast.24, s32[3,32]{1,0:T(4,128)} %counts_ref.3, bf16[3,32,256,128]{3,2,1,0:T(8,128)(2,1)} %bitcast.22, bf16[200,4096]{1,0:T(8,128)(2,1)} %e_ref.3, ...), custom_call_target="tpu_custom_call" | custom-call | flops 6710886400 | bytes 4194304 | tf_op jit(solution)/shard_map/fold/pallas_call | solution.py:205
  15.5 1.2 %collective-permute-done.2.others_ref = bf16[32,1600]{1,0:T(8,128)(2,1)S(1)} collective-permute-done((bf16[32,1600]{1,0:T(8,128)(2,1)S(1)}, bf16[32,1600]{1,0:T(8,128)(2,1)S(1)}, u32[]{:S(2)}, u32[]{:S(2)}) %collective-permute-start.2) | collective-permute-done | bytes 102432 | tf_op jit(solution)/shard_map/ppermute | solution.py:323
  16.7 1.0 %far.1 = (f32[4,48,600]{2,1,0:T(8,128)S(1)}, f32[4,48,600]{2,1,0:T(8,128)S(1)}) custom-call(f32[1152,200]{1,0:T(8,128)S(1)} %get-tuple-element.16.near_ref, bf16[2,8,32,384]{3,2,1,0:T(8,128)(2,1)S(1)} %collective-permute-done.1.tiles, bf16[256,384]{1,0:T(8,128)(2,1)S(1)} %get-tuple-element.18.kept, bf16[2,768,512]{2,1,0:T(8,128)(2,1)S(1)} %get-tuple-element.19.a_ref, ...), custom_call_target="tpu_custom_call" | custom-call | tf_op jit(solution)/shard_map/far/pallas_call | solution.py:272
  17.7 0.1 collective-permute-start.3
  17.8 1.9 %collective-permute-done.3 = f32[4,48,600]{2,1,0:T(8,128)S(1)} collective-permute-done((f32[4,48,600]{2,1,0:T(8,128)S(1)}, f32[4,48,600]{2,1,0:T(8,128)S(1)}, u32[]{:S(2)}, u32[]{:S(2)}) %collective-permute-start.3) | collective-permute-done | bytes 460832 | tf_op jit(solution)/shard_map/ppermute | solution.py:326
  19.6 0.1 fusion.3
  19.7 1.9 %collective-permute-start.4 = (bf16[48,600]{1,0:T(8,128)(2,1)S(1)}, bf16[48,600]{1,0:T(8,128)(2,1)S(1)}, u32[]{:S(2)}, u32[]{:S(2)}) collective-permute-start(bf16[48,600]{1,0:T(8,128)(2,1)S(1)} %get-tuple-element.25), channel_id=1, source_target_pairs={{0,6},{1,7},{2,4},{3,5},{4,2},{5,3},{6,0},{7,1},{8,14},{9,15},{10,... | collective-permute-start | bytes 172808 | tf_op jit(solution)/shard_map/ppermute | solution.py:330
  21.6 1.1 %collective-permute-start.6 = (bf16[48,600]{1,0:T(8,128)(2,1)S(1)}, bf16[48,600]{1,0:T(8,128)(2,1)S(1)}, u32[]{:S(2)}, u32[]{:S(2)}) collective-permute-start(bf16[48,600]{1,0:T(8,128)(2,1)S(1)} %get-tuple-element.26), channel_id=1, source_target_pairs={{0,2},{1,3},{2,0},{3,1},{4,6},{5,7},{6,4},{7,5},{8,10},{9,11},{10,... | collective-permute-start | bytes 172808 | tf_op jit(solution)/shard_map/ppermute | solution.py:330
  22.8 0.5 %collective-permute-start.5 = (bf16[48,600]{1,0:T(8,128)(2,1)S(1)}, bf16[48,600]{1,0:T(8,128)(2,1)S(1)}, u32[]{:S(2)}, u32[]{:S(2)}) collective-permute-start(bf16[48,600]{1,0:T(8,128)(2,1)S(1)} %get-tuple-element.27), channel_id=1, source_target_pairs={{0,4},{1,5},{2,6},{3,7},{4,0},{5,1},{6,2},{7,3},{8,12},{9,13},{10,... | collective-permute-start | bytes 172808 | tf_op jit(solution)/shard_map/ppermute | solution.py:330
  23.3 1.6 %collective-permute-done.4 = bf16[48,600]{1,0:T(8,128)(2,1)S(1)} collective-permute-done((bf16[48,600]{1,0:T(8,128)(2,1)S(1)}, bf16[48,600]{1,0:T(8,128)(2,1)S(1)}, u32[]{:S(2)}, u32[]{:S(2)}) %collective-permute-start.4) | collective-permute-done | bytes 57632 | tf_op jit(solution)/shard_map/ppermute | solution.py:330
  24.9 1.4 %collective-permute-done.6 = bf16[48,600]{1,0:T(8,128)(2,1)S(1)} collective-permute-done((bf16[48,600]{1,0:T(8,128)(2,1)S(1)}, bf16[48,600]{1,0:T(8,128)(2,1)S(1)}, u32[]{:S(2)}, u32[]{:S(2)}) %collective-permute-start.6) | collective-permute-done | bytes 57632 | tf_op jit(solution)/shard_map/ppermute | solution.py:330
  26.3 0.7 %collective-permute-done.5 = bf16[48,600]{1,0:T(8,128)(2,1)S(1)} collective-permute-done((bf16[48,600]{1,0:T(8,128)(2,1)S(1)}, bf16[48,600]{1,0:T(8,128)(2,1)S(1)}, u32[]{:S(2)}, u32[]{:S(2)}) %collective-permute-start.5) | collective-permute-done | bytes 57632 | tf_op jit(solution)/shard_map/ppermute | solution.py:330
  27.1 2.3 %collective-permute-start.9 = (f32[12,600]{1,0:T(8,128)S(1)}, f32[12,600]{1,0:T(8,128)S(1)}, u32[]{:S(2)}, u32[]{:S(2)}) collective-permute-start(f32[12,600]{1,0:T(8,128)S(1)} %get-tuple-element.28), channel_id=1, source_target_pairs={{0,8},{8,0},{16,24},{24,16},{1,9},{9,1},{17,25},{25,17},{2,10},{10... | collective-permute-start | bytes 86408 | tf_op jit(solution)/shard_map/ppermute | solution.py:336
  29.3 2.6 %collective-permute-start.8 = (f32[12,600]{1,0:T(8,128)S(1)}, f32[12,600]{1,0:T(8,128)S(1)}, u32[]{:S(2)}, u32[]{:S(2)}) collective-permute-start(f32[12,600]{1,0:T(8,128)S(1)} %get-tuple-element.29), channel_id=1, source_target_pairs={{0,16},{8,24},{16,0},{24,8},{1,17},{9,25},{17,1},{25,9},{2,18},{10... | collective-permute-start | bytes 86408 | tf_op jit(solution)/shard_map/ppermute | solution.py:336
  31.9 3.2 %collective-permute-done.8.refs_2_ = f32[12,600]{1,0:T(8,128)S(1)} collective-permute-done((f32[12,600]{1,0:T(8,128)S(1)}, f32[12,600]{1,0:T(8,128)S(1)}, u32[]{:S(2)}, u32[]{:S(2)}) %collective-permute-start.8) | collective-permute-done | bytes 28832 | tf_op jit(solution)/shard_map/ppermute | solution.py:336
  35.1 2.6 %collective-permute-done.7.refs_1_ = f32[12,600]{1,0:T(8,128)S(1)} collective-permute-done((f32[12,600]{1,0:T(8,128)S(1)}, f32[12,600]{1,0:T(8,128)S(1)}, u32[]{:S(2)}, u32[]{:S(2)}) %collective-permute-start.7) | collective-permute-done | bytes 28832 | tf_op jit(solution)/shard_map/ppermute | solution.py:336
  37.7 0.7 %finish.1 = f32[36,200]{1,0:T(8,128)} custom-call(f32[12,600]{1,0:T(8,128)S(1)} %get-tuple-element.31.refs_0_, f32[12,600]{1,0:T(8,128)S(1)} %collective-permute-done.7.refs_1_, f32[12,600]{1,0:T(8,128)S(1)} %collective-permute-done.8.refs_2_, f32[12,600]{1,0:T(8,128)S(1)} %collective-permute-done.9.refs_3_), custom_call_target="tpu_custom_call" | custom-call | tf_op jit(solution)/shard_map/finish/pallas_call | solution.py:297
  (7 shorter events, 0.1 us)
Async XLA Ops:
  0.0 1.5 %copy-start = (bf16[3,16,32,384]{3,2,1,0:T(8,128)(2,1)S(1)}, bf16[3,16,32,384]{3,2,1,0:T(8,128)(2,1)}, u32[]{:S(2)}) copy-start(bf16[3,16,32,384]{3,2,1,0:T(8,128)(2,1)} %rest_0_.1) | copy-start | bytes 3538948
  1.5 7.8 %collective-permute-start = (bf16[3,16,32,384]{3,2,1,0:T(8,128)(2,1)S(1)}, bf16[3,16,32,384]{3,2,1,0:T(8,128)(2,1)S(1)}, u32[]{:S(2)}, u32[]{:S(2)}) collective-permute-start(bf16[3,16,32,384]{3,2,1,0:T(8,128)(2,1)S(1)} %copy-done), channel_id=1, source_target_pairs={{0,1},{1,0},{2,3},{3,2},{4,5},{5,4},{6,7},{7,6},{8,9},{9,8},{10,11... | collective-permute-start | bytes 3538952 | tf_op jit(solution)/shard_map/ppermute | solution.py:318
  2.0 14.7 %collective-permute-start.1 = (bf16[2,8,32,384]{3,2,1,0:T(8,128)(2,1)S(1)}, bf16[2,8,32,384]{3,2,1,0:T(8,128)(2,1)S(1)}, u32[]{:S(2)}, u32[]{:S(2)}) collective-permute-start(bf16[2,8,32,384]{3,2,1,0:T(8,128)(2,1)S(1)} %pick.1), channel_id=1, source_target_pairs={{0,7},{1,2},{2,1},{3,4},{4,3},{5,6},{6,5},{7,0},{8,15},{9,10},{10,... | collective-permute-start | bytes 1179656 | tf_op jit(solution)/shard_map/ppermute | solution.py:317
  9.2 7.5 %collective-permute-start.2 = (bf16[32,1600]{1,0:T(8,128)(2,1)S(1)}, bf16[32,1600]{1,0:T(8,128)(2,1)S(1)}, u32[]{:S(2)}, u32[]{:S(2)}) collective-permute-start(bf16[32,1600]{1,0:T(8,128)(2,1)S(1)} %get-tuple-element.20), channel_id=1, source_target_pairs={{0,7},{1,2},{2,1},{3,4},{4,3},{5,6},{6,5},{7,0},{8,15},{9,10},{10,... | collective-permute-start | bytes 307208 | tf_op jit(solution)/shard_map/ppermute | solution.py:323
  17.7 1.9 %collective-permute-start.3 = (f32[4,48,600]{2,1,0:T(8,128)S(1)}, f32[4,48,600]{2,1,0:T(8,128)S(1)}, u32[]{:S(2)}, u32[]{:S(2)}) collective-permute-start(f32[4,48,600]{2,1,0:T(8,128)S(1)} %get-tuple-element.22), channel_id=1, source_target_pairs={{0,1},{1,0},{2,3},{3,2},{4,5},{5,4},{6,7},{7,6},{8,9},{9,8},{10,11... | collective-permute-start | bytes 1382408 | tf_op jit(solution)/shard_map/ppermute | solution.py:326
  19.7 5.2 %collective-permute-start.4 = (bf16[48,600]{1,0:T(8,128)(2,1)S(1)}, bf16[48,600]{1,0:T(8,128)(2,1)S(1)}, u32[]{:S(2)}, u32[]{:S(2)}) collective-permute-start(bf16[48,600]{1,0:T(8,128)(2,1)S(1)} %get-tuple-element.25), channel_id=1, source_target_pairs={{0,6},{1,7},{2,4},{3,5},{4,2},{5,3},{6,0},{7,1},{8,14},{9,15},{10,... | collective-permute-start | bytes 172808 | tf_op jit(solution)/shard_map/ppermute | solution.py:330
  21.6 4.6 %collective-permute-start.6 = (bf16[48,600]{1,0:T(8,128)(2,1)S(1)}, bf16[48,600]{1,0:T(8,128)(2,1)S(1)}, u32[]{:S(2)}, u32[]{:S(2)}) collective-permute-start(bf16[48,600]{1,0:T(8,128)(2,1)S(1)} %get-tuple-element.26), channel_id=1, source_target_pairs={{0,2},{1,3},{2,0},{3,1},{4,6},{5,7},{6,4},{7,5},{8,10},{9,11},{10,... | collective-permute-start | bytes 172808 | tf_op jit(solution)/shard_map/ppermute | solution.py:330
  22.8 4.2 %collective-permute-start.5 = (bf16[48,600]{1,0:T(8,128)(2,1)S(1)}, bf16[48,600]{1,0:T(8,128)(2,1)S(1)}, u32[]{:S(2)}, u32[]{:S(2)}) collective-permute-start(bf16[48,600]{1,0:T(8,128)(2,1)S(1)} %get-tuple-element.27), channel_id=1, source_target_pairs={{0,4},{1,5},{2,6},{3,7},{4,0},{5,1},{6,2},{7,3},{8,12},{9,13},{10,... | collective-permute-start | bytes 172808 | tf_op jit(solution)/shard_map/ppermute | solution.py:330
  27.1 4.9 %collective-permute-start.9 = (f32[12,600]{1,0:T(8,128)S(1)}, f32[12,600]{1,0:T(8,128)S(1)}, u32[]{:S(2)}, u32[]{:S(2)}) collective-permute-start(f32[12,600]{1,0:T(8,128)S(1)} %get-tuple-element.28), channel_id=1, source_target_pairs={{0,8},{8,0},{16,24},{24,16},{1,9},{9,1},{17,25},{25,17},{2,10},{10... | collective-permute-start | bytes 86408 | tf_op jit(solution)/shard_map/ppermute | solution.py:336
  29.3 5.8 %collective-permute-start.8 = (f32[12,600]{1,0:T(8,128)S(1)}, f32[12,600]{1,0:T(8,128)S(1)}, u32[]{:S(2)}, u32[]{:S(2)}) collective-permute-start(f32[12,600]{1,0:T(8,128)S(1)} %get-tuple-element.29), channel_id=1, source_target_pairs={{0,16},{8,24},{16,0},{24,8},{1,17},{9,25},{17,1},{25,9},{2,18},{10... | collective-permute-start | bytes 86408 | tf_op jit(solution)/shard_map/ppermute | solution.py:336
  31.9 5.8 %collective-permute-start.7 = (f32[12,600]{1,0:T(8,128)S(1)}, f32[12,600]{1,0:T(8,128)S(1)}, u32[]{:S(2)}, u32[]{:S(2)}) collective-permute-start(f32[12,600]{1,0:T(8,128)S(1)} %get-tuple-element.30), channel_id=1, source_target_pairs={{0,24},{8,16},{16,8},{24,0},{1,25},{9,17},{17,9},{25,1},{2,26},{10... | collective-permute-start | bytes 86408 | tf_op jit(solution)/shard_map/ppermute | solution.py:336

commit v6 on v5

--- a/solution.py
+++ b/solution.py
@@ -226,7 +226,7 @@
 
 
 def far_kernel(
-    lat_count, near_ref, tiles, kept, a_ref, others_ref, keep_ref, send_ref, rows_of, whole, units
+    lat_count, near_ref, tiles, kept, a_ref, others_ref, keep_ref, send_ref, rows_of, units
 ):
     lat, lon, _, _, _, lon_count = place()
     grids, cap, cells, columns = tiles.shape[0] + 1, *tiles.shape[1:]
@@ -248,9 +248,11 @@
         product = near_ref[part, :] + total
         product = product.reshape(columns // MONTHS, MONTHS, eofs)
         product = product - jnp.mean(product, axis=1, keepdims=True)
-        whole[part, :] = product.reshape(columns, eofs)
-    for u in range(units.shape[0]):
-        units[u] = whole[u * rows : (u + 1) * rows, :]
+        product = product.reshape(columns, eofs)
+        for u in range(part.start // rows, pl.cdiv(part.stop, rows)):
+            low, high = max(part.start, u * rows), min(part.stop, (u + 1) * rows)
+            piece = product[low - part.start : high - part.start, :]
+            units[u, low - u * rows : high - u * rows, :] = piece
     plane, core = lax.div(lon, CORES), lax.rem(lon, CORES)
     for c, out in ((0, keep_ref), (1, send_ref)):
         for r in range(planes):
@@ -276,7 +278,6 @@
         out_specs=(VMEM, VMEM),
         scratch_shapes=[
             pltpu.VMEM((kept.shape[0], eofs), others.dtype),
-            pltpu.VMEM((total_columns, eofs), jnp.float32),
             pltpu.VMEM((lat_count * lon_count, rows, eofs), jnp.float32),
         ],
         compiler_params=grant(16),

time: 38.6 us -> 38.5 us (level)
  no operation moved by 1% of the time
where the time goes in v6:
time: 38.5 us; the launch traced here: 38.4 us
  Pallas kernels  12.7 us (33%)
  starting transfers between devices  12.6 us (33%)
  waiting for transfers between devices  12.6 us (33%)
    pallas_call x2, Pallas kernels, fold(): pl.pallas_call(functools.partial(fold_kernel, src_tiles, first, sends), o...  9.8 us
    ppermute x3, waiting for transfers between devices, shards(): parts.append(lax.ppermute(plane_sum[q * rows:(q + 1) * rows], 'lat', swap))  5.8 us
    ppermute x3, starting transfers between devices, shards(): parts.append(lax.ppermute(plane_sum[q * rows:(q + 1) * rows], 'lat', swap))  4.88 us
    ppermute x3, waiting for transfers between devices, shards(): sent = lax.ppermute(pair_sum[r].astype(jnp.bfloat16), 'lon', swap)  3.71 us
    ppermute x3, starting transfers between devices, shards(): sent = lax.ppermute(pair_sum[r].astype(jnp.bfloat16), 'lon', swap)  3.55 us
    ppermute x1, starting transfers between devices, shards(): tiles = lax.ppermute(picked, 'lon', off_chip)  3.54 us
    ppermute x1, waiting for transfers between devices, shards(): pair_sum = keep + lax.ppermute(send, 'lon', on_chip)  1.85 us
    pallas_call x1, Pallas kernels, pick(): pl.pallas_call(pick_kernel, out_shape=jax.ShapeDtypeStruct((grids, cap, c...  1.25 us
  transfers between devices with their start and end apart: 10, of which 7 were waited for; matrix products, arithmetic and copies ran while one was open for 0% of the time, Pallas kernels for 26%

profile of v6, /device:TPU:0, one launch (start us, length us, event | category | flops | bytes accessed | tf_op | source)
XLA Modules:
  0.0 38.4 jit_solution(12510115575396060122)
XLA Ops:
  0.0 1.3 %pick.1 = bf16[2,8,32,384]{3,2,1,0:T(8,128)(2,1)S(1)} custom-call(s32[3,16,32]{2,1,0:T(8,128)} %bitcast.18, bf16[3,16,32,384]{3,2,1,0:T(8,128)(2,1)} %rest_0_.1), custom_call_target="tpu_custom_call" | custom-call | tf_op jit(solution)/shard_map/pick/pallas_call | solution.py:69
  1.3 0.2 copy-done
  1.5 0.5 %collective-permute-start = (bf16[3,16,32,384]{3,2,1,0:T(8,128)(2,1)S(1)}, bf16[3,16,32,384]{3,2,1,0:T(8,128)(2,1)S(1)}, u32[]{:S(2)}, u32[]{:S(2)}) collective-permute-start(bf16[3,16,32,384]{3,2,1,0:T(8,128)(2,1)S(1)} %copy-done), channel_id=1, source_target_pairs={{0,1},{1,0},{2,3},{3,2},{4,5},{5,4},{6,7},{7,6},{8,9},{9,8},{10,11... | collective-permute-start | bytes 3538952 | tf_op jit(solution)/shard_map/ppermute | solution.py:319
  2.0 3.5 %collective-permute-start.1 = (bf16[2,8,32,384]{3,2,1,0:T(8,128)(2,1)S(1)}, bf16[2,8,32,384]{3,2,1,0:T(8,128)(2,1)S(1)}, u32[]{:S(2)}, u32[]{:S(2)}) collective-permute-start(bf16[2,8,32,384]{3,2,1,0:T(8,128)(2,1)S(1)} %pick.1), channel_id=1, source_target_pairs={{0,7},{1,2},{2,1},{3,4},{4,3},{5,6},{6,5},{7,0},{8,15},{9,10},{10,... | collective-permute-start | bytes 1179656 | tf_op jit(solution)/shard_map/ppermute | solution.py:318
  5.5 3.6 %fold.2 = (bf16[1,768,512]{2,1,0:T(8,128)(2,1)S(1)}, bf16[32,1600]{1,0:T(8,128)(2,1)S(1)}) custom-call(s32[3,16,32]{2,1,0:T(8,128)} %bitcast.19, s32[3,8,32]{2,1,0:T(8,128)} %bitcast.23, s32[3,32]{1,0:T(4,128)} %counts_ref.3, bf16[3,32,256,128]{3,2,1,0:T(8,128)(2,1)} %bitcast.21, bf16[200,4096]{1,0:T(8,128)(2,1)} %e_ref.3), custom_call_target="tpu_custom_call" | custom-call | flops 3355443200 | bytes 2097152 | tf_op jit(solution)/shard_map/fold/pallas_call | solution.py:205
  9.2 0.1 collective-permute-start.2
  9.3 0.0 collective-permute-done.rest_1_
  9.3 6.2 %fold.3 = (bf16[2,768,512]{2,1,0:T(8,128)(2,1)S(1)}, f32[1152,200]{1,0:T(8,128)S(1)}, bf16[256,384]{1,0:T(8,128)(2,1)S(1)}) custom-call(s32[3,16,32]{2,1,0:T(8,128)} %bitcast.20, s32[3,8,32]{2,1,0:T(8,128)} %bitcast.24, s32[3,32]{1,0:T(4,128)} %counts_ref.3, bf16[3,32,256,128]{3,2,1,0:T(8,128)(2,1)} %bitcast.22, bf16[200,4096]{1,0:T(8,128)(2,1)} %e_ref.3, ...), custom_call_target="tpu_custom_call" | custom-call | flops 6710886400 | bytes 4194304 | tf_op jit(solution)/shard_map/fold/pallas_call | solution.py:205
  15.5 1.2 %collective-permute-done.2.others_ref = bf16[32,1600]{1,0:T(8,128)(2,1)S(1)} collective-permute-done((bf16[32,1600]{1,0:T(8,128)(2,1)S(1)}, bf16[32,1600]{1,0:T(8,128)(2,1)S(1)}, u32[]{:S(2)}, u32[]{:S(2)}) %collective-permute-start.2) | collective-permute-done | bytes 102432 | tf_op jit(solution)/shard_map/ppermute | solution.py:324
  16.7 0.9 %far.1 = (f32[4,48,600]{2,1,0:T(8,128)S(1)}, f32[4,48,600]{2,1,0:T(8,128)S(1)}) custom-call(f32[1152,200]{1,0:T(8,128)S(1)} %get-tuple-element.16.near_ref, bf16[2,8,32,384]{3,2,1,0:T(8,128)(2,1)S(1)} %collective-permute-done.1.tiles, bf16[256,384]{1,0:T(8,128)(2,1)S(1)} %get-tuple-element.18.kept, bf16[2,768,512]{2,1,0:T(8,128)(2,1)S(1)} %get-tuple-element.19.a_ref, ...), custom_call_target="tpu_custom_call" | custom-call | tf_op jit(solution)/shard_map/far/pallas_call | solution.py:274
  17.6 0.1 collective-permute-start.3
  17.7 1.9 %collective-permute-done.3 = f32[4,48,600]{2,1,0:T(8,128)S(1)} collective-permute-done((f32[4,48,600]{2,1,0:T(8,128)S(1)}, f32[4,48,600]{2,1,0:T(8,128)S(1)}, u32[]{:S(2)}, u32[]{:S(2)}) %collective-permute-start.3) | collective-permute-done | bytes 460832 | tf_op jit(solution)/shard_map/ppermute | solution.py:327
  19.5 0.1 fusion.3
  19.7 1.9 %collective-permute-start.4 = (bf16[48,600]{1,0:T(8,128)(2,1)S(1)}, bf16[48,600]{1,0:T(8,128)(2,1)S(1)}, u32[]{:S(2)}, u32[]{:S(2)}) collective-permute-start(bf16[48,600]{1,0:T(8,128)(2,1)S(1)} %get-tuple-element.25), channel_id=1, source_target_pairs={{0,6},{1,7},{2,4},{3,5},{4,2},{5,3},{6,0},{7,1},{8,14},{9,15},{10,... | collective-permute-start | bytes 172808 | tf_op jit(solution)/shard_map/ppermute | solution.py:331
  21.6 1.1 %collective-permute-start.6 = (bf16[48,600]{1,0:T(8,128)(2,1)S(1)}, bf16[48,600]{1,0:T(8,128)(2,1)S(1)}, u32[]{:S(2)}, u32[]{:S(2)}) collective-permute-start(bf16[48,600]{1,0:T(8,128)(2,1)S(1)} %get-tuple-element.26), channel_id=1, source_target_pairs={{0,2},{1,3},{2,0},{3,1},{4,6},{5,7},{6,4},{7,5},{8,10},{9,11},{10,... | collective-permute-start | bytes 172808 | tf_op jit(solution)/shard_map/ppermute | solution.py:331
  22.7 0.5 %collective-permute-start.5 = (bf16[48,600]{1,0:T(8,128)(2,1)S(1)}, bf16[48,600]{1,0:T(8,128)(2,1)S(1)}, u32[]{:S(2)}, u32[]{:S(2)}) collective-permute-start(bf16[48,600]{1,0:T(8,128)(2,1)S(1)} %get-tuple-element.27), channel_id=1, source_target_pairs={{0,4},{1,5},{2,6},{3,7},{4,0},{5,1},{6,2},{7,3},{8,12},{9,13},{10,... | collective-permute-start | bytes 172808 | tf_op jit(solution)/shard_map/ppermute | solution.py:331
  23.2 1.6 %collective-permute-done.4 = bf16[48,600]{1,0:T(8,128)(2,1)S(1)} collective-permute-done((bf16[48,600]{1,0:T(8,128)(2,1)S(1)}, bf16[48,600]{1,0:T(8,128)(2,1)S(1)}, u32[]{:S(2)}, u32[]{:S(2)}) %collective-permute-start.4) | collective-permute-done | bytes 57632 | tf_op jit(solution)/shard_map/ppermute | solution.py:331
  24.8 1.4 %collective-permute-done.6 = bf16[48,600]{1,0:T(8,128)(2,1)S(1)} collective-permute-done((bf16[48,600]{1,0:T(8,128)(2,1)S(1)}, bf16[48,600]{1,0:T(8,128)(2,1)S(1)}, u32[]{:S(2)}, u32[]{:S(2)}) %collective-permute-start.6) | collective-permute-done | bytes 57632 | tf_op jit(solution)/shard_map/ppermute | solution.py:331
  26.2 0.7 %collective-permute-done.5 = bf16[48,600]{1,0:T(8,128)(2,1)S(1)} collective-permute-done((bf16[48,600]{1,0:T(8,128)(2,1)S(1)}, bf16[48,600]{1,0:T(8,128)(2,1)S(1)}, u32[]{:S(2)}, u32[]{:S(2)}) %collective-permute-start.5) | collective-permute-done | bytes 57632 | tf_op jit(solution)/shard_map/ppermute | solution.py:331
  27.0 2.3 %collective-permute-start.9 = (f32[12,600]{1,0:T(8,128)S(1)}, f32[12,600]{1,0:T(8,128)S(1)}, u32[]{:S(2)}, u32[]{:S(2)}) collective-permute-start(f32[12,600]{1,0:T(8,128)S(1)} %get-tuple-element.28), channel_id=1, source_target_pairs={{0,8},{8,0},{16,24},{24,16},{1,9},{9,1},{17,25},{25,17},{2,10},{10... | collective-permute-start | bytes 86408 | tf_op jit(solution)/shard_map/ppermute | solution.py:337
  29.3 2.6 %collective-permute-start.8 = (f32[12,600]{1,0:T(8,128)S(1)}, f32[12,600]{1,0:T(8,128)S(1)}, u32[]{:S(2)}, u32[]{:S(2)}) collective-permute-start(f32[12,600]{1,0:T(8,128)S(1)} %get-tuple-element.29), channel_id=1, source_target_pairs={{0,16},{8,24},{16,0},{24,8},{1,17},{9,25},{17,1},{25,9},{2,18},{10... | collective-permute-start | bytes 86408 | tf_op jit(solution)/shard_map/ppermute | solution.py:337
  31.9 3.2 %collective-permute-done.8.refs_2_ = f32[12,600]{1,0:T(8,128)S(1)} collective-permute-done((f32[12,600]{1,0:T(8,128)S(1)}, f32[12,600]{1,0:T(8,128)S(1)}, u32[]{:S(2)}, u32[]{:S(2)}) %collective-permute-start.8) | collective-permute-done | bytes 28832 | tf_op jit(solution)/shard_map/ppermute | solution.py:337
  35.0 2.6 %collective-permute-done.7.refs_1_ = f32[12,600]{1,0:T(8,128)S(1)} collective-permute-done((f32[12,600]{1,0:T(8,128)S(1)}, f32[12,600]{1,0:T(8,128)S(1)}, u32[]{:S(2)}, u32[]{:S(2)}) %collective-permute-start.7) | collective-permute-done | bytes 28832 | tf_op jit(solution)/shard_map/ppermute | solution.py:337
  37.7 0.7 %finish.1 = f32[36,200]{1,0:T(8,128)} custom-call(f32[12,600]{1,0:T(8,128)S(1)} %get-tuple-element.31.refs_0_, f32[12,600]{1,0:T(8,128)S(1)} %collective-permute-done.7.refs_1_, f32[12,600]{1,0:T(8,128)S(1)} %collective-permute-done.8.refs_2_, f32[12,600]{1,0:T(8,128)S(1)} %collective-permute-done.9.refs_3_), custom_call_target="tpu_custom_call" | custom-call | tf_op jit(solution)/shard_map/finish/pallas_call | solution.py:298
  (7 shorter events, 0.1 us)
Async XLA Ops:
  0.0 1.5 %copy-start = (bf16[3,16,32,384]{3,2,1,0:T(8,128)(2,1)S(1)}, bf16[3,16,32,384]{3,2,1,0:T(8,128)(2,1)}, u32[]{:S(2)}) copy-start(bf16[3,16,32,384]{3,2,1,0:T(8,128)(2,1)} %rest_0_.1) | copy-start | bytes 3538948
  1.5 7.8 %collective-permute-start = (bf16[3,16,32,384]{3,2,1,0:T(8,128)(2,1)S(1)}, bf16[3,16,32,384]{3,2,1,0:T(8,128)(2,1)S(1)}, u32[]{:S(2)}, u32[]{:S(2)}) collective-permute-start(bf16[3,16,32,384]{3,2,1,0:T(8,128)(2,1)S(1)} %copy-done), channel_id=1, source_target_pairs={{0,1},{1,0},{2,3},{3,2},{4,5},{5,4},{6,7},{7,6},{8,9},{9,8},{10,11... | collective-permute-start | bytes 3538952 | tf_op jit(solution)/shard_map/ppermute | solution.py:319
  2.0 14.7 %collective-permute-start.1 = (bf16[2,8,32,384]{3,2,1,0:T(8,128)(2,1)S(1)}, bf16[2,8,32,384]{3,2,1,0:T(8,128)(2,1)S(1)}, u32[]{:S(2)}, u32[]{:S(2)}) collective-permute-start(bf16[2,8,32,384]{3,2,1,0:T(8,128)(2,1)S(1)} %pick.1), channel_id=1, source_target_pairs={{0,7},{1,2},{2,1},{3,4},{4,3},{5,6},{6,5},{7,0},{8,15},{9,10},{10,... | collective-permute-start | bytes 1179656 | tf_op jit(solution)/shard_map/ppermute | solution.py:318
  9.2 7.5 %collective-permute-start.2 = (bf16[32,1600]{1,0:T(8,128)(2,1)S(1)}, bf16[32,1600]{1,0:T(8,128)(2,1)S(1)}, u32[]{:S(2)}, u32[]{:S(2)}) collective-permute-start(bf16[32,1600]{1,0:T(8,128)(2,1)S(1)} %get-tuple-element.20), channel_id=1, source_target_pairs={{0,7},{1,2},{2,1},{3,4},{4,3},{5,6},{6,5},{7,0},{8,15},{9,10},{10,... | collective-permute-start | bytes 307208 | tf_op jit(solution)/shard_map/ppermute | solution.py:324
  17.6 1.9 %collective-permute-start.3 = (f32[4,48,600]{2,1,0:T(8,128)S(1)}, f32[4,48,600]{2,1,0:T(8,128)S(1)}, u32[]{:S(2)}, u32[]{:S(2)}) collective-permute-start(f32[4,48,600]{2,1,0:T(8,128)S(1)} %get-tuple-element.22), channel_id=1, source_target_pairs={{0,1},{1,0},{2,3},{3,2},{4,5},{5,4},{6,7},{7,6},{8,9},{9,8},{10,11... | collective-permute-start | bytes 1382408 | tf_op jit(solution)/shard_map/ppermute | solution.py:327
  19.7 5.2 %collective-permute-start.4 = (bf16[48,600]{1,0:T(8,128)(2,1)S(1)}, bf16[48,600]{1,0:T(8,128)(2,1)S(1)}, u32[]{:S(2)}, u32[]{:S(2)}) collective-permute-start(bf16[48,600]{1,0:T(8,128)(2,1)S(1)} %get-tuple-element.25), channel_id=1, source_target_pairs={{0,6},{1,7},{2,4},{3,5},{4,2},{5,3},{6,0},{7,1},{8,14},{9,15},{10,... | collective-permute-start | bytes 172808 | tf_op jit(solution)/shard_map/ppermute | solution.py:331
  21.6 4.6 %collective-permute-start.6 = (bf16[48,600]{1,0:T(8,128)(2,1)S(1)}, bf16[48,600]{1,0:T(8,128)(2,1)S(1)}, u32[]{:S(2)}, u32[]{:S(2)}) collective-permute-start(bf16[48,600]{1,0:T(8,128)(2,1)S(1)} %get-tuple-element.26), channel_id=1, source_target_pairs={{0,2},{1,3},{2,0},{3,1},{4,6},{5,7},{6,4},{7,5},{8,10},{9,11},{10,... | collective-permute-start | bytes 172808 | tf_op jit(solution)/shard_map/ppermute | solution.py:331
  22.7 4.2 %collective-permute-start.5 = (bf16[48,600]{1,0:T(8,128)(2,1)S(1)}, bf16[48,600]{1,0:T(8,128)(2,1)S(1)}, u32[]{:S(2)}, u32[]{:S(2)}) collective-permute-start(bf16[48,600]{1,0:T(8,128)(2,1)S(1)} %get-tuple-element.27), channel_id=1, source_target_pairs={{0,4},{1,5},{2,6},{3,7},{4,0},{5,1},{6,2},{7,3},{8,12},{9,13},{10,... | collective-permute-start | bytes 172808 | tf_op jit(solution)/shard_map/ppermute | solution.py:331
  27.0 4.9 %collective-permute-start.9 = (f32[12,600]{1,0:T(8,128)S(1)}, f32[12,600]{1,0:T(8,128)S(1)}, u32[]{:S(2)}, u32[]{:S(2)}) collective-permute-start(f32[12,600]{1,0:T(8,128)S(1)} %get-tuple-element.28), channel_id=1, source_target_pairs={{0,8},{8,0},{16,24},{24,16},{1,9},{9,1},{17,25},{25,17},{2,10},{10... | collective-permute-start | bytes 86408 | tf_op jit(solution)/shard_map/ppermute | solution.py:337
  29.3 5.8 %collective-permute-start.8 = (f32[12,600]{1,0:T(8,128)S(1)}, f32[12,600]{1,0:T(8,128)S(1)}, u32[]{:S(2)}, u32[]{:S(2)}) collective-permute-start(f32[12,600]{1,0:T(8,128)S(1)} %get-tuple-element.29), channel_id=1, source_target_pairs={{0,16},{8,24},{16,0},{24,8},{1,17},{9,25},{17,1},{25,9},{2,18},{10... | collective-permute-start | bytes 86408 | tf_op jit(solution)/shard_map/ppermute | solution.py:337
  31.9 5.8 %collective-permute-start.7 = (f32[12,600]{1,0:T(8,128)S(1)}, f32[12,600]{1,0:T(8,128)S(1)}, u32[]{:S(2)}, u32[]{:S(2)}) collective-permute-start(f32[12,600]{1,0:T(8,128)S(1)} %get-tuple-element.30), channel_id=1, source_target_pairs={{0,24},{8,16},{16,8},{24,0},{1,25},{9,17},{17,9},{25,1},{2,26},{10... | collective-permute-start | bytes 86408 | tf_op jit(solution)/shard_map/ppermute | solution.py:337
